TPU v7x, 64 devices: a 2x2x8 block of a 4x4x8 slice. The times are simulated.
64 devices in a mesh: dp: 4 (over x, y), ctx: 16 (over z, core).
Axes of the slice: x: 2, y: 2, z: 8, core: 2. Of those that a mesh axis runs over, the one named last changes fastest.
The devices are a block of a 4x4x8 slice.
Arguments:
- x_chunk: bfloat16 [32768, 1152], P(('dp', 'ctx')), parts along dimension 0
- cache_len: int32 [4], P('dp'), parts along dimension 0
- k_cache: bfloat16 [2, 32768, 1, 256], P(None, ('dp', 'ctx')), parts along dimension 1
- v_cache: bfloat16 [2, 32768, 1, 256], P(None, ('dp', 'ctx')), parts along dimension 1
- k_local: bfloat16 [2, 2048, 1, 256], P(None, 'dp'), parts along dimension 1
- v_local: bfloat16 [2, 2048, 1, 256], P(None, 'dp'), parts along dimension 1
- g_attn: bfloat16 [4, 1152], replicated
- g_mlp: bfloat16 [4, 1152], replicated
- w_q: bfloat16 [4, 1152, 1024], replicated
- w_k: bfloat16 [4, 1152, 256], replicated
- w_v: bfloat16 [4, 1152, 256], replicated
- w_o: bfloat16 [4, 1024, 1152], replicated
- w_gate: bfloat16 [4, 1152, 6912], replicated
- w_up: bfloat16 [4, 1152, 6912], replicated
- w_down: bfloat16 [4, 6912, 1152], replicated
Outputs:
- output: bfloat16 [32768, 1152], P(('dp', 'ctx')), parts along dimension 0
There are 4 independent parts. A program takes and returns all parts, laid end to end along the dimension named above; an argument that names none is the same for every part.
All inputs are finite; a program needn't handle non-finite values.
Results may differ from a plain program's by a relative error of at most 0.02.
Values are sent between devices in bfloat16 or wider.
A program may use at most 768 MiB of HBM per device.

v0:
```python
import jax
import jax.numpy as jnp
from jax import lax
from jax.sharding import PartitionSpec as P, NamedSharding

QUERY_ROWS = 128
NORM_EPS = 1e-6


def rms_norm(rows_in, gain_vec):
    rows_f32 = rows_in.astype(jnp.float32)
    inv_rms = lax.rsqrt(jnp.mean(rows_f32 * rows_f32, axis=-1, keepdims=True) + NORM_EPS)
    return (rows_f32 * inv_rms * gain_vec.astype(jnp.float32)).astype(jnp.bfloat16)


def project(rows_in, weight):
    return jnp.dot(rows_in, weight, preferred_element_type=jnp.float32).astype(jnp.bfloat16)


def qkv_heads(normed, w_query, w_key, w_value, kv_heads, head_dim):
    lead_dims = normed.shape[:-1]
    groups = w_query.shape[-1] // (kv_heads * head_dim)
    queries = project(normed, w_query).reshape(lead_dims + (kv_heads, groups, head_dim))
    new_k = project(normed, w_key).reshape(lead_dims + (kv_heads, head_dim))
    new_v = project(normed, w_value).reshape(lead_dims + (kv_heads, head_dim))
    return queries, new_k, new_v


def add_residual(hidden, attn_out, w_out):
    return (hidden.astype(jnp.float32) + jnp.dot(attn_out, w_out, preferred_element_type=jnp.float32)).astype(jnp.bfloat16)


def mlp_block(hidden, gain_vec, w_gate, w_up, w_down):
    normed = rms_norm(hidden, gain_vec)
    gate_pre = jnp.dot(normed, w_gate, preferred_element_type=jnp.float32)
    up_pre = jnp.dot(normed, w_up, preferred_element_type=jnp.float32)
    act_bf16 = (jax.nn.gelu(gate_pre, approximate=True) * up_pre).astype(jnp.bfloat16)
    return (hidden.astype(jnp.float32) + jnp.dot(act_bf16, w_down, preferred_element_type=jnp.float32)).astype(jnp.bfloat16)


def band_attention(queries, ext_k, ext_v):
    n_rows, kv_heads, groups, head_dim = queries.shape
    window = ext_k.shape[0] - n_rows
    blocks = n_rows // window
    score_scale = head_dim ** -0.5
    q_blocks = queries.reshape(blocks, window, kv_heads, groups, head_dim)
    k_blocks = ext_k.reshape(blocks + 1, window, kv_heads, head_dim)
    v_blocks = ext_v.reshape(blocks + 1, window, kv_heads, head_dim)
    row_ids = lax.broadcasted_iota(jnp.int32, (window, window), 0)
    col_ids = lax.broadcasted_iota(jnp.int32, (window, window), 1)
    prev_scores = jnp.einsum('bqhgd,bkhd->bhgqk', q_blocks, k_blocks[:-1], preferred_element_type=jnp.float32) * score_scale
    prev_scores = jnp.where(col_ids > row_ids, prev_scores, -jnp.inf)
    own_scores = jnp.einsum('bqhgd,bkhd->bhgqk', q_blocks, k_blocks[1:], preferred_element_type=jnp.float32) * score_scale
    own_scores = jnp.where(col_ids <= row_ids, own_scores, -jnp.inf)
    row_max = jnp.maximum(prev_scores.max(axis=-1), own_scores.max(axis=-1))[..., None]
    prev_probs = jnp.exp(prev_scores - row_max)
    own_probs = jnp.exp(own_scores - row_max)
    row_sum = prev_probs.sum(axis=-1) + own_probs.sum(axis=-1)
    weighted = (jnp.einsum('bhgqk,bkhd->bqhgd', prev_probs.astype(jnp.bfloat16), v_blocks[:-1], preferred_element_type=jnp.float32)
                + jnp.einsum('bhgqk,bkhd->bqhgd', own_probs.astype(jnp.bfloat16), v_blocks[1:], preferred_element_type=jnp.float32))
    out_rows = weighted / jnp.transpose(row_sum, (0, 3, 1, 2))[..., None]
    return out_rows.astype(jnp.bfloat16).reshape(n_rows, kv_heads * groups * head_dim)


def global_attention(queries, cache_k, cache_v, new_k, new_v, valid_len, first_row):
    n_rows, kv_heads, groups, head_dim = queries.shape
    score_scale = head_dim ** -0.5
    cache_mask = jnp.arange(cache_k.shape[0]) < valid_len
    new_pos = jnp.arange(new_k.shape[0])

    def one_block(block_idx):
        row_start = block_idx * QUERY_ROWS
        q_rows = lax.dynamic_slice_in_dim(queries, row_start, QUERY_ROWS, axis=0)
        q_pos = first_row + row_start + jnp.arange(QUERY_ROWS)
        cache_scores = jnp.einsum('qhgd,khd->hgqk', q_rows, cache_k, preferred_element_type=jnp.float32) * score_scale
        cache_scores = jnp.where(cache_mask, cache_scores, -jnp.inf)
        new_scores = jnp.einsum('qhgd,khd->hgqk', q_rows, new_k, preferred_element_type=jnp.float32) * score_scale
        new_scores = jnp.where(new_pos[None, :] <= q_pos[:, None], new_scores, -jnp.inf)
        row_max = jnp.maximum(cache_scores.max(axis=-1), new_scores.max(axis=-1))[..., None]
        cache_probs = jnp.exp(cache_scores - row_max)
        new_probs = jnp.exp(new_scores - row_max)
        row_sum = cache_probs.sum(axis=-1) + new_probs.sum(axis=-1)
        weighted = (jnp.einsum('hgqk,khd->qhgd', cache_probs.astype(jnp.bfloat16), cache_v, preferred_element_type=jnp.float32)
                    + jnp.einsum('hgqk,khd->qhgd', new_probs.astype(jnp.bfloat16), new_v, preferred_element_type=jnp.float32))
        return (weighted / jnp.transpose(row_sum, (2, 0, 1))[..., None]).astype(jnp.bfloat16)

    out_blocks = lax.map(one_block, jnp.arange(n_rows // QUERY_ROWS))
    return out_blocks.reshape(n_rows, kv_heads * groups * head_dim)


def solution(mesh):
    ctx_size = mesh.shape['ctx']
    shift_pairs = [(src_dev, src_dev + 1) for src_dev in range(ctx_size - 1)]
    row_spec = P(('dp', 'ctx'), None)
    cache_spec = P(None, ('dp', 'ctx'), None, None)
    local_spec = P(None, 'dp', None, None)
    in_specs = (row_spec, P('dp'), cache_spec, cache_spec, local_spec, local_spec) + (P(),) * 9

    def device_step(x_rows, cache_len, k_cache, v_cache, k_local, v_local, g_attn, g_mlp, w_q, w_k, w_v, w_o, w_gate, w_up, w_down):
        dev_idx = lax.axis_index('ctx')
        is_first = dev_idx == 0
        n_rows = x_rows.shape[0]
        window = k_local.shape[1]
        kv_heads = k_local.shape[2]
        head_dim = k_local.shape[3]
        valid_len = cache_len[0]
        hidden = x_rows
        for pair_idx in range(k_cache.shape[0]):
            layer_idx = 2 * pair_idx
            queries, new_k, new_v = qkv_heads(rms_norm(hidden, g_attn[layer_idx]), w_q[layer_idx], w_k[layer_idx], w_v[layer_idx], kv_heads, head_dim)
            halo_k = lax.ppermute(new_k[n_rows - window:], 'ctx', shift_pairs)
            halo_v = lax.ppermute(new_v[n_rows - window:], 'ctx', shift_pairs)
            halo_k = jnp.where(is_first, k_local[pair_idx], halo_k)
            halo_v = jnp.where(is_first, v_local[pair_idx], halo_v)
            attn_out = band_attention(queries, jnp.concatenate([halo_k, new_k], axis=0), jnp.concatenate([halo_v, new_v], axis=0))
            hidden = add_residual(hidden, attn_out, w_o[layer_idx])
            hidden = mlp_block(hidden, g_mlp[layer_idx], w_gate[layer_idx], w_up[layer_idx], w_down[layer_idx])
            layer_idx = 2 * pair_idx + 1
            queries, new_k, new_v = qkv_heads(rms_norm(hidden, g_attn[layer_idx]), w_q[layer_idx], w_k[layer_idx], w_v[layer_idx], kv_heads, head_dim)
            all_k = lax.all_gather(new_k, 'ctx', axis=0, tiled=True)
            all_v = lax.all_gather(new_v, 'ctx', axis=0, tiled=True)
            cache_k = lax.all_gather(k_cache[pair_idx], 'ctx', axis=0, tiled=True)
            cache_v = lax.all_gather(v_cache[pair_idx], 'ctx', axis=0, tiled=True)
            attn_out = global_attention(queries, cache_k, cache_v, all_k, all_v, valid_len, dev_idx * n_rows)
            hidden = add_residual(hidden, attn_out, w_o[layer_idx])
            hidden = mlp_block(hidden, g_mlp[layer_idx], w_gate[layer_idx], w_up[layer_idx], w_down[layer_idx])
        return hidden

    return jax.shard_map(device_step, mesh=mesh, in_specs=in_specs, out_specs=row_spec, check_vma=False)
```

profile of v0, /device:TPU:21, one launch (start us, length us, event | category | flops | bytes accessed | tf_op | source)
XLA Modules:
  0.0 736.4 jit_solution(2176305037929115989)
XLA Ops:
  40.8 16.6 %fusion.114 = f32[512,6912]{1,0:T(8,128)} fusion(bf16[4,1152,6912]{2,1,0:T(8,128)(2,1)} %param.31, bf16[512,1152]{1,0:T(8,128)(2,1)S(1)} %get-tuple-element.282, f32[1152]{0:T(1024)S(1)} %get-tuple-element.215, f32[512]{0:T(512)S(1)} %add_rsqrt_fusion.6), kind=kOutput, calls=%fused_computation.92 | convolution fusion | flops 8156086272 | bytes 31267328 | tf_op jit(solution)/shard_map/dot_general | solution.py:35
  57.4 17.6 %fusion.136.clone.5.clone.5 = bf16[512,6912]{1,0:T(8,128)(2,1)} fusion(f32[512,6912]{1,0:T(8,128)} %fusion.114, bf16[4,1152,6912]{2,1,0:T(8,128)(2,1)} %param.32, bf16[512,1152]{1,0:T(8,128)(2,1)S(1)} %get-tuple-element.282, f32[1152]{0:T(1024)S(1)} %get-tuple-element.215, f32[512]{0:T(512)S(1)} %add_rsqrt_fusion.6), kind=kOutput, calls=%fused_computation.114.clone.clone.clone.clone.clone.clone.clone.clone.clone.2 | convolution fusion | flops 8191475712 | bytes 38345216 | tf_op jit(solution)/shard_map/dot_general | solution.py:36
  75.0 14.8 %fusion.254 = (f32[512]{0:T(512)S(1)}, bf16[512,1152]{1,0:T(8,128)(2,1)S(1)}) fusion(bf16[4,6912,1152]{2,1,0:T(8,128)(2,1)} %param.33, bf16[512,1152]{1,0:T(8,128)(2,1)} %copy-done.23, bf16[512,6912]{1,0:T(8,128)(2,1)} %fusion.136.clone.5.clone.5), kind=kOutput, calls=%fused_computation.216 | convolution fusion | flops 8157265408 | bytes 25364480 | tf_op jit(solution)/shard_map/dot_general | solution.py:38
  100.8 36.6 %all-gather.23.cloned.1.call-done = bf16[8192,256]{1,0:T(8,128)(2,1)} async-done(((bf16[512,256]{1,0:T(8,128)(2,1)}), bf16[8192,256]{1,0:T(8,128)(2,1)}) %all-gather.23.cloned.1.call-update) | async-done | bytes 4194320 | tf_op jit(solution)/shard_map/all_gather | solution.py:121
  137.4 38.4 %all-gather.19.cloned.1.call-done = bf16[8192,256]{1,0:T(8,128)(2,1)} async-done(((bf16[512,256]{1,0:T(8,128)(2,1)}), bf16[8192,256]{1,0:T(8,128)(2,1)}) %all-gather.19.cloned.1.call-update) | async-done | bytes 4194320 | tf_op jit(solution)/shard_map/all_gather | solution.py:120
  176.0 152.1 %while.22 = (s32[]{:T(128)}, bf16[4,128,1,4,256]{4,3,1,0,2:T(4,128)(2,1)S(1)}, s32[4]{0:T(128)S(1)}, bf16[512,1,4,256]{3,2,0,1:T(4,128)(2,1)S(1)}, bf16[8192,1,2...) while((s32[]{:T(128)}, ...), condition=%wide.region_12.13_spmd.clone, body=%wide.region_7.12_spmd.clone.sunk | while | flops 8650103808 | bytes 139244800 | solution.py:87
  183.6 9.3 %fusion.526 = (f32[4,128]{1,0:T(4,128)S(1)}, f32[1,4,128,8192]{3,2,1,0:T(8,128)}) fusion(bf16[8192,1,256]{2,0,1:T(8,128)(2,1)} %get-tuple-element.479, bf16[128,1,4,256]{3,2,0,1:T(4,128)(2,1)S(1)} %constant_dynamic-slice_fusion.4, pred[8192]{0:T(1024)(128)(4,1)S(1)} %iota_compare_fusion.11), kind=kOutput, calls=%fused_computation.402.clone.1 | convolution fusion | flops 2160066048 | bytes 21243904 | tf_op jit(solution)/shard_map/while/body/eval_jaxpr/qhgd,khd->hgqk/dot_general | solution.py:75
  204.3 9.4 %fusion.529 = bf16[1,128,1,4,256]{4,1,3,2,0:T(8,128)(2,1)S(1)} fusion(f32[4,128,256]{2,1,0:T(8,128)S(1)} %fusion.527, bf16[8192,1,256]{2,0,1:T(8,128)(2,1)} %get-tuple-element.482, f32[1,4,128,8192]{3,2,1,0:T(8,128)} %get-tuple-element.428, f32[4,128]{1,0:T(4,128)S(1)} %max.42, f32[128,4]{0,1:T(4,128)S(1)} %add_bitcast_fusion.6), kind=kOutput, calls=%fused_computation.28.clone.1 | convolution fusion | flops 2156265472 | bytes 21762048 | tf_op jit(solution)/shard_map/while/body/eval_jaxpr/hgqk,khd->qhgd/dot_general | solution.py:83
  221.5 9.3 %fusion.526 = (f32[4,128]{1,0:T(4,128)S(1)}, f32[1,4,128,8192]{3,2,1,0:T(8,128)}) fusion(bf16[8192,1,256]{2,0,1:T(8,128)(2,1)} %get-tuple-element.479, bf16[128,1,4,256]{3,2,0,1:T(4,128)(2,1)S(1)} %constant_dynamic-slice_fusion.4, pred[8192]{0:T(1024)(128)(4,1)S(1)} %iota_compare_fusion.11), kind=kOutput, calls=%fused_computation.402.clone.1 | convolution fusion | flops 2160066048 | bytes 21243904 | tf_op jit(solution)/shard_map/while/body/eval_jaxpr/qhgd,khd->hgqk/dot_general | solution.py:75
  242.2 9.4 %fusion.529 = bf16[1,128,1,4,256]{4,1,3,2,0:T(8,128)(2,1)S(1)} fusion(f32[4,128,256]{2,1,0:T(8,128)S(1)} %fusion.527, bf16[8192,1,256]{2,0,1:T(8,128)(2,1)} %get-tuple-element.482, f32[1,4,128,8192]{3,2,1,0:T(8,128)} %get-tuple-element.428, f32[4,128]{1,0:T(4,128)S(1)} %max.42, f32[128,4]{0,1:T(4,128)S(1)} %add_bitcast_fusion.6), kind=kOutput, calls=%fused_computation.28.clone.1 | convolution fusion | flops 2156265472 | bytes 21762048 | tf_op jit(solution)/shard_map/while/body/eval_jaxpr/hgqk,khd->qhgd/dot_general | solution.py:83
  259.5 9.3 %fusion.526 = (f32[4,128]{1,0:T(4,128)S(1)}, f32[1,4,128,8192]{3,2,1,0:T(8,128)}) fusion(bf16[8192,1,256]{2,0,1:T(8,128)(2,1)} %get-tuple-element.479, bf16[128,1,4,256]{3,2,0,1:T(4,128)(2,1)S(1)} %constant_dynamic-slice_fusion.4, pred[8192]{0:T(1024)(128)(4,1)S(1)} %iota_compare_fusion.11), kind=kOutput, calls=%fused_computation.402.clone.1 | convolution fusion | flops 2160066048 | bytes 21243904 | tf_op jit(solution)/shard_map/while/body/eval_jaxpr/qhgd,khd->hgqk/dot_general | solution.py:75
  280.2 9.4 %fusion.529 = bf16[1,128,1,4,256]{4,1,3,2,0:T(8,128)(2,1)S(1)} fusion(f32[4,128,256]{2,1,0:T(8,128)S(1)} %fusion.527, bf16[8192,1,256]{2,0,1:T(8,128)(2,1)} %get-tuple-element.482, f32[1,4,128,8192]{3,2,1,0:T(8,128)} %get-tuple-element.428, f32[4,128]{1,0:T(4,128)S(1)} %max.42, f32[128,4]{0,1:T(4,128)S(1)} %add_bitcast_fusion.6), kind=kOutput, calls=%fused_computation.28.clone.1 | convolution fusion | flops 2156265472 | bytes 21762048 | tf_op jit(solution)/shard_map/while/body/eval_jaxpr/hgqk,khd->qhgd/dot_general | solution.py:83
  297.4 9.3 %fusion.526 = (f32[4,128]{1,0:T(4,128)S(1)}, f32[1,4,128,8192]{3,2,1,0:T(8,128)}) fusion(bf16[8192,1,256]{2,0,1:T(8,128)(2,1)} %get-tuple-element.479, bf16[128,1,4,256]{3,2,0,1:T(4,128)(2,1)S(1)} %constant_dynamic-slice_fusion.4, pred[8192]{0:T(1024)(128)(4,1)S(1)} %iota_compare_fusion.11), kind=kOutput, calls=%fused_computation.402.clone.1 | convolution fusion | flops 2160066048 | bytes 21243904 | tf_op jit(solution)/shard_map/while/body/eval_jaxpr/qhgd,khd->hgqk/dot_general | solution.py:75
  318.1 9.4 %fusion.529 = bf16[1,128,1,4,256]{4,1,3,2,0:T(8,128)(2,1)S(1)} fusion(f32[4,128,256]{2,1,0:T(8,128)S(1)} %fusion.527, bf16[8192,1,256]{2,0,1:T(8,128)(2,1)} %get-tuple-element.482, f32[1,4,128,8192]{3,2,1,0:T(8,128)} %get-tuple-element.428, f32[4,128]{1,0:T(4,128)S(1)} %max.42, f32[128,4]{0,1:T(4,128)S(1)} %add_bitcast_fusion.6), kind=kOutput, calls=%fused_computation.28.clone.1 | convolution fusion | flops 2156265472 | bytes 21762048 | tf_op jit(solution)/shard_map/while/body/eval_jaxpr/hgqk,khd->qhgd/dot_general | solution.py:83
  332.0 16.2 %fusion.108 = f32[512,6912]{1,0:T(8,128)} fusion(bf16[4,1152,6912]{2,1,0:T(8,128)(2,1)} %param.31, bf16[512,1152]{1,0:T(8,128)(2,1)S(1)} %get-tuple-element.286, f32[1152]{0:T(1024)S(1)} %copy-done.11, f32[512]{0:T(512)S(1)} %add_rsqrt_fusion.4), kind=kOutput, calls=%fused_computation.86 | convolution fusion | flops 8156086272 | bytes 31267328 | tf_op jit(solution)/shard_map/dot_general | solution.py:35
  348.2 17.5 %fusion.145.clone.5.clone.5 = bf16[512,6912]{1,0:T(8,128)(2,1)} fusion(f32[512,6912]{1,0:T(8,128)} %fusion.108, bf16[4,1152,6912]{2,1,0:T(8,128)(2,1)} %param.32, bf16[512,1152]{1,0:T(8,128)(2,1)S(1)} %get-tuple-element.286, f32[1152]{0:T(1024)S(1)} %copy-done.11, f32[512]{0:T(512)S(1)} %add_rsqrt_fusion.4), kind=kOutput, calls=%fused_computation.123.clone.clone.clone.clone.clone.clone.clone.clone.clone.2 | convolution fusion | flops 8191475712 | bytes 38345216 | tf_op jit(solution)/shard_map/dot_general | solution.py:36
  365.7 14.7 %fusion.260 = (f32[512]{0:T(512)S(1)}, bf16[512,1152]{1,0:T(8,128)(2,1)S(1)}) fusion(bf16[4,6912,1152]{2,1,0:T(8,128)(2,1)} %param.33, bf16[512,1152]{1,0:T(8,128)(2,1)S(1)} %get-tuple-element.286, bf16[512,6912]{1,0:T(8,128)(2,1)} %fusion.145.clone.5.clone.5), kind=kOutput, calls=%fused_computation.222 | convolution fusion | flops 8157265408 | bytes 25364480 | tf_op jit(solution)/shard_map/dot_general | solution.py:38
  402.3 16.6 %fusion.102 = f32[512,6912]{1,0:T(8,128)} fusion(bf16[4,1152,6912]{2,1,0:T(8,128)(2,1)} %param.31, bf16[512,1152]{1,0:T(8,128)(2,1)S(1)} %get-tuple-element.294, f32[1152]{0:T(1024)S(1)} %copy-done.9, f32[512]{0:T(512)S(1)} %add_rsqrt_fusion.2), kind=kOutput, calls=%fused_computation.80 | convolution fusion | flops 8156086272 | bytes 31267328 | tf_op jit(solution)/shard_map/dot_general | solution.py:35
  419.0 17.8 %fusion.154.clone.5.clone.5 = bf16[512,6912]{1,0:T(8,128)(2,1)} fusion(f32[512,6912]{1,0:T(8,128)} %fusion.102, bf16[4,1152,6912]{2,1,0:T(8,128)(2,1)} %param.32, bf16[512,1152]{1,0:T(8,128)(2,1)S(1)} %get-tuple-element.294, f32[1152]{0:T(1024)S(1)} %copy-done.9, f32[512]{0:T(512)S(1)} %add_rsqrt_fusion.2), kind=kOutput, calls=%fused_computation.132.clone.clone.clone.clone.clone.clone.clone.clone.clone.2 | convolution fusion | flops 8191475712 | bytes 38345216 | tf_op jit(solution)/shard_map/dot_general | solution.py:36
  436.8 14.8 %fusion.266 = (f32[512]{0:T(512)S(1)}, bf16[512,1152]{1,0:T(8,128)(2,1)S(1)}) fusion(bf16[4,6912,1152]{2,1,0:T(8,128)(2,1)} %param.33, bf16[512,1152]{1,0:T(8,128)(2,1)} %copy-done.22, bf16[512,6912]{1,0:T(8,128)(2,1)} %fusion.154.clone.5.clone.5), kind=kOutput, calls=%fused_computation.228 | convolution fusion | flops 8157265408 | bytes 25364480 | tf_op jit(solution)/shard_map/dot_general | solution.py:38
  459.8 32.6 %all-gather.31.cloned.1.call-done = bf16[8192,256]{1,0:T(8,128)(2,1)} async-done(((bf16[512,256]{1,0:T(8,128)(2,1)}), bf16[8192,256]{1,0:T(8,128)(2,1)}) %all-gather.31.cloned.1.call-update) | async-done | bytes 4194320 | tf_op jit(solution)/shard_map/all_gather | solution.py:121
  492.4 38.5 %all-gather.27.cloned.1.call-done = bf16[8192,256]{1,0:T(8,128)(2,1)} async-done(((bf16[512,256]{1,0:T(8,128)(2,1)}), bf16[8192,256]{1,0:T(8,128)(2,1)}) %all-gather.27.cloned.1.call-update) | async-done | bytes 4194320 | tf_op jit(solution)/shard_map/all_gather | solution.py:120
  531.2 151.7 %while.23 = (s32[]{:T(128)}, bf16[4,128,1,4,256]{4,3,1,0,2:T(4,128)(2,1)S(1)}, s32[4]{0:T(128)S(1)}, bf16[512,1,4,256]{3,2,0,1:T(4,128)(2,1)S(1)}, bf16[8192,1,2...) while((s32[]{:T(128)}, ...), condition=%wide.region_26.27_spmd.clone, body=%wide.region_21.26_spmd.clone.sunk | while | flops 8650103808 | bytes 139244800 | solution.py:87
  538.8 9.3 %fusion.535 = (f32[4,128]{1,0:T(4,128)S(1)}, f32[1,4,128,8192]{3,2,1,0:T(8,128)}) fusion(bf16[8192,1,256]{2,0,1:T(8,128)(2,1)} %get-tuple-element.521, bf16[128,1,4,256]{3,2,0,1:T(4,128)(2,1)S(1)} %constant_dynamic-slice_fusion.5, pred[8192]{0:T(1024)(128)(4,1)S(1)} %iota_compare_fusion.13), kind=kOutput, calls=%fused_computation.404.clone.1 | convolution fusion | flops 2160066048 | bytes 21243904 | tf_op jit(solution)/shard_map/while/body/eval_jaxpr/qhgd,khd->hgqk/dot_general | solution.py:75
  559.5 9.4 %fusion.538 = bf16[1,128,1,4,256]{4,1,3,2,0:T(8,128)(2,1)S(1)} fusion(f32[4,128,256]{2,1,0:T(8,128)S(1)} %fusion.536, bf16[8192,1,256]{2,0,1:T(8,128)(2,1)} %get-tuple-element.524, f32[1,4,128,8192]{3,2,1,0:T(8,128)} %get-tuple-element.444, f32[4,128]{1,0:T(4,128)S(1)} %max.43, f32[128,4]{0,1:T(4,128)S(1)} %add_bitcast_fusion.7), kind=kOutput, calls=%fused_computation.59.clone.1 | convolution fusion | flops 2156265472 | bytes 21762048 | tf_op jit(solution)/shard_map/while/body/eval_jaxpr/hgqk,khd->qhgd/dot_general | solution.py:83
  576.7 9.3 %fusion.535 = (f32[4,128]{1,0:T(4,128)S(1)}, f32[1,4,128,8192]{3,2,1,0:T(8,128)}) fusion(bf16[8192,1,256]{2,0,1:T(8,128)(2,1)} %get-tuple-element.521, bf16[128,1,4,256]{3,2,0,1:T(4,128)(2,1)S(1)} %constant_dynamic-slice_fusion.5, pred[8192]{0:T(1024)(128)(4,1)S(1)} %iota_compare_fusion.13), kind=kOutput, calls=%fused_computation.404.clone.1 | convolution fusion | flops 2160066048 | bytes 21243904 | tf_op jit(solution)/shard_map/while/body/eval_jaxpr/qhgd,khd->hgqk/dot_general | solution.py:75
  597.3 9.4 %fusion.538 = bf16[1,128,1,4,256]{4,1,3,2,0:T(8,128)(2,1)S(1)} fusion(f32[4,128,256]{2,1,0:T(8,128)S(1)} %fusion.536, bf16[8192,1,256]{2,0,1:T(8,128)(2,1)} %get-tuple-element.524, f32[1,4,128,8192]{3,2,1,0:T(8,128)} %get-tuple-element.444, f32[4,128]{1,0:T(4,128)S(1)} %max.43, f32[128,4]{0,1:T(4,128)S(1)} %add_bitcast_fusion.7), kind=kOutput, calls=%fused_computation.59.clone.1 | convolution fusion | flops 2156265472 | bytes 21762048 | tf_op jit(solution)/shard_map/while/body/eval_jaxpr/hgqk,khd->qhgd/dot_general | solution.py:83
  635.2 9.4 %fusion.538 = bf16[1,128,1,4,256]{4,1,3,2,0:T(8,128)(2,1)S(1)} fusion(f32[4,128,256]{2,1,0:T(8,128)S(1)} %fusion.536, bf16[8192,1,256]{2,0,1:T(8,128)(2,1)} %get-tuple-element.524, f32[1,4,128,8192]{3,2,1,0:T(8,128)} %get-tuple-element.444, f32[4,128]{1,0:T(4,128)S(1)} %max.43, f32[128,4]{0,1:T(4,128)S(1)} %add_bitcast_fusion.7), kind=kOutput, calls=%fused_computation.59.clone.1 | convolution fusion | flops 2156265472 | bytes 21762048 | tf_op jit(solution)/shard_map/while/body/eval_jaxpr/hgqk,khd->qhgd/dot_general | solution.py:83
  652.4 9.3 %fusion.535 = (f32[4,128]{1,0:T(4,128)S(1)}, f32[1,4,128,8192]{3,2,1,0:T(8,128)}) fusion(bf16[8192,1,256]{2,0,1:T(8,128)(2,1)} %get-tuple-element.521, bf16[128,1,4,256]{3,2,0,1:T(4,128)(2,1)S(1)} %constant_dynamic-slice_fusion.5, pred[8192]{0:T(1024)(128)(4,1)S(1)} %iota_compare_fusion.13), kind=kOutput, calls=%fused_computation.404.clone.1 | convolution fusion | flops 2160066048 | bytes 21243904 | tf_op jit(solution)/shard_map/while/body/eval_jaxpr/qhgd,khd->hgqk/dot_general | solution.py:75
  673.1 9.4 %fusion.538 = bf16[1,128,1,4,256]{4,1,3,2,0:T(8,128)(2,1)S(1)} fusion(f32[4,128,256]{2,1,0:T(8,128)S(1)} %fusion.536, bf16[8192,1,256]{2,0,1:T(8,128)(2,1)} %get-tuple-element.524, f32[1,4,128,8192]{3,2,1,0:T(8,128)} %get-tuple-element.444, f32[4,128]{1,0:T(4,128)S(1)} %max.43, f32[128,4]{0,1:T(4,128)S(1)} %add_bitcast_fusion.7), kind=kOutput, calls=%fused_computation.59.clone.1 | convolution fusion | flops 2156265472 | bytes 21762048 | tf_op jit(solution)/shard_map/while/body/eval_jaxpr/hgqk,khd->qhgd/dot_general | solution.py:83
  686.8 16.2 %fusion.96 = f32[512,6912]{1,0:T(8,128)} fusion(bf16[4,1152,6912]{2,1,0:T(8,128)(2,1)} %param.31, bf16[512,1152]{1,0:T(8,128)(2,1)S(1)} %get-tuple-element.298, f32[1152]{0:T(1024)S(1)} %copy-done.7, f32[512]{0:T(512)S(1)} %add_rsqrt_fusion), kind=kOutput, calls=%fused_computation.74 | convolution fusion | flops 8156086272 | bytes 31267328 | tf_op jit(solution)/shard_map/dot_general | solution.py:35
  703.0 26.3 %fusion.239 = bf16[512,1152]{1,0:T(8,128)(2,1)} fusion(bf16[4,6912,1152]{2,1,0:T(8,128)(2,1)} %param.33, f32[512,6912]{1,0:T(8,128)} %fusion.96, bf16[4,1152,6912]{2,1,0:T(8,128)(2,1)} %param.32, bf16[512,1152]{1,0:T(8,128)(2,1)S(1)} %get-tuple-element.298, f32[1152]{0:T(1024)S(1)} %copy-done.7, f32[512]{0:T(512)S(1)} %add_rsqrt_fusion), kind=kOutput, calls=%fused_computation.205 | convolution fusion | flops 16346972160 | bytes 49555456 | tf_op jit(solution)/shard_map/dot_general | solution.py:38
  (229 shorter events, 240.6 us)
Async XLA Ops:
  6.5 12.3 %copy-start.4 = (bf16[512,1152]{1,0:T(8,128)(2,1)S(1)}, bf16[512,1152]{1,0:T(8,128)(2,1)}, u32[]{:S(2)}) copy-start(bf16[512,1152]{1,0:T(8,128)(2,1)} %param.19) | copy-start | bytes 3538948
  6.5 94.2 %all-gather.17.cloned.1.call-start = ((), (), s32[]{:S(2)}) async-start(), calls=%async_computation | async-start | bytes 4456448 | tf_op jit(solution)/shard_map/all_gather | solution.py:122
  8.6 13.9 %copy-start.5 = (bf16[2,512,1,256]{3,1,2,0:T(8,128)(2,1)S(1)}, bf16[2,512,1,256]{3,1,2,0:T(8,128)(2,1)}, u32[]{:S(2)}) copy-start(bf16[2,512,1,256]{3,1,2,0:T(8,128)(2,1)} %param.22) | copy-start | bytes 1572868
  8.6 92.2 %all-gather.21.cloned.1.call-start = ((), (), s32[]{:S(2)}) async-start(), calls=%async_computation.2 | async-start | bytes 4456448 | tf_op jit(solution)/shard_map/all_gather | solution.py:123
  13.7 17.7 %collective-permute-start.1 = (bf16[512,1,256]{2,0,1:T(8,128)(2,1)S(1)}, bf16[512,1,256]{2,0,1:T(8,128)(2,1)S(1)}, u32[]{:S(2)}, u32[]{:S(2)}) collective-permute-start(bf16[512,1,256]{2,0,1:T(8,128)(2,1)S(1)} %bitcast.628), channel_id=1, source_target_pairs={{0,1},{1,2},{2,3},{3,4},{4,5},{5,6},{6,7},{7,8},{8,9},{9,10},{10,1... | collective-permute-start | bytes 786440 | tf_op jit(solution)/shard_map/ppermute | solution.py:111
  20.5 15.2 %collective-permute-start = (bf16[512,1,256]{2,0,1:T(8,128)(2,1)S(1)}, bf16[512,1,256]{2,0,1:T(8,128)(2,1)S(1)}, u32[]{:S(2)}, u32[]{:S(2)}) collective-permute-start(bf16[512,1,256]{2,0,1:T(8,128)(2,1)S(1)} %bitcast.627), channel_id=1, source_target_pairs={{0,1},{1,2},{2,3},{3,4},{4,5},{5,6},{6,7},{7,8},{8,9},{9,10},{10,1... | collective-permute-start | bytes 786440 | tf_op jit(solution)/shard_map/ppermute | solution.py:112
  23.4 114.0 %all-gather.23.cloned.1.call-start = ((), (), s32[]{:S(2)}) async-start(), calls=%async_computation.3 | async-start | bytes 4456448 | tf_op jit(solution)/shard_map/all_gather | solution.py:121
  24.2 10.1 %copy-start.2 = (pred[512,512]{0,1:T(8,128)(4,1)}, pred[512,512]{0,1:T(8,128)(4,1)S(1)}, u32[]{:S(2)}) copy-start(pred[512,512]{0,1:T(8,128)(4,1)S(1)} %get-tuple-element.299) | copy-start | bytes 786436
  24.2 11.5 %copy-start = (pred[512,512]{0,1:T(8,128)(4,1)}, pred[512,512]{0,1:T(8,128)(4,1)S(1)}, u32[]{:S(2)}) copy-start(pred[512,512]{0,1:T(8,128)(4,1)S(1)} %get-tuple-element.300) | copy-start | bytes 786436
  40.7 16.7 %copy-start.23 = (bf16[512,1152]{1,0:T(8,128)(2,1)}, bf16[512,1152]{1,0:T(8,128)(2,1)S(1)}, u32[]{:S(2)}) copy-start(bf16[512,1152]{1,0:T(8,128)(2,1)S(1)} %get-tuple-element.282) | copy-start | bytes 3538948
  89.8 9.9 %copy-start.20 = (bf16[512,1152]{1,0:T(8,128)(2,1)}, bf16[512,1152]{1,0:T(8,128)(2,1)S(1)}, u32[]{:S(2)}) copy-start(bf16[512,1152]{1,0:T(8,128)(2,1)S(1)} %get-tuple-element.284) | copy-start | bytes 3538948
  92.6 83.1 %all-gather.19.cloned.1.call-start = ((), (), s32[]{:S(2)}) async-start(), calls=%async_computation.1 | async-start | bytes 4456448 | tf_op jit(solution)/shard_map/all_gather | solution.py:120
  95.1 364.6 %all-gather.25.cloned.1.call-start = ((), (), s32[]{:S(2)}) async-start(), calls=%async_computation.4 | async-start | bytes 4456448 | tf_op jit(solution)/shard_map/all_gather | solution.py:122
  95.8 364.0 %all-gather.29.cloned.1.call-start = ((), (), s32[]{:S(2)}) async-start(), calls=%async_computation.6 | async-start | bytes 4456448 | tf_op jit(solution)/shard_map/all_gather | solution.py:123
  96.4 396.0 %all-gather.31.cloned.1.call-start = ((), (), s32[]{:S(2)}) async-start(), calls=%async_computation.7 | async-start | bytes 4456448 | tf_op jit(solution)/shard_map/all_gather | solution.py:121
  192.9 8.8 %copy-start.12 = (bf16[8192,1,256]{2,0,1:T(8,128)(2,1)S(1)}, bf16[8192,1,256]{2,0,1:T(8,128)(2,1)}, u32[]{:S(2)}) copy-start(bf16[8192,1,256]{2,0,1:T(8,128)(2,1)} %get-tuple-element.483) | copy-start | bytes 12582916 | tf_op jit(solution)/shard_map/while
  230.9 8.8 %copy-start.12 = (bf16[8192,1,256]{2,0,1:T(8,128)(2,1)S(1)}, bf16[8192,1,256]{2,0,1:T(8,128)(2,1)}, u32[]{:S(2)}) copy-start(bf16[8192,1,256]{2,0,1:T(8,128)(2,1)} %get-tuple-element.483) | copy-start | bytes 12582916 | tf_op jit(solution)/shard_map/while
  268.8 8.8 %copy-start.12 = (bf16[8192,1,256]{2,0,1:T(8,128)(2,1)S(1)}, bf16[8192,1,256]{2,0,1:T(8,128)(2,1)}, u32[]{:S(2)}) copy-start(bf16[8192,1,256]{2,0,1:T(8,128)(2,1)} %get-tuple-element.483) | copy-start | bytes 12582916 | tf_op jit(solution)/shard_map/while
  306.7 8.8 %copy-start.12 = (bf16[8192,1,256]{2,0,1:T(8,128)(2,1)S(1)}, bf16[8192,1,256]{2,0,1:T(8,128)(2,1)}, u32[]{:S(2)}) copy-start(bf16[8192,1,256]{2,0,1:T(8,128)(2,1)} %get-tuple-element.483) | copy-start | bytes 12582916 | tf_op jit(solution)/shard_map/while
  365.7 14.7 %copy-start.10 = (f32[1152]{0:T(1024)S(1)}, f32[1152]{0:T(1024)}, u32[]{:S(2)}) copy-start(f32[1152]{0:T(1024)} %get-tuple-element.220) | copy-start | bytes 13828
  382.2 9.6 %copy-start.3 = (pred[512,512]{0,1:T(8,128)(4,1)S(1)}, pred[512,512]{0,1:T(8,128)(4,1)}, u32[]{:S(2)}) copy-start(pred[512,512]{0,1:T(8,128)(4,1)} %copy-done.2) | copy-start | bytes 786436
  386.2 6.7 copy-start.1
  386.2 6.7 collective-permute-start.3
  389.6 7.7 %collective-permute-start.2 = (bf16[512,1,256]{2,0,1:T(8,128)(2,1)S(1)}, bf16[512,1,256]{2,0,1:T(8,128)(2,1)S(1)}, u32[]{:S(2)}, u32[]{:S(2)}) collective-permute-start(bf16[512,1,256]{2,0,1:T(8,128)(2,1)S(1)} %bitcast.629), channel_id=1, source_target_pairs={{0,1},{1,2},{2,3},{3,4},{4,5},{5,6},{6,7},{7,8},{8,9},{9,10},{10,1... | collective-permute-start | bytes 786440 | tf_op jit(solution)/shard_map/ppermute | solution.py:112
  402.3 16.7 %copy-start.22 = (bf16[512,1152]{1,0:T(8,128)(2,1)}, bf16[512,1152]{1,0:T(8,128)(2,1)S(1)}, u32[]{:S(2)}) copy-start(bf16[512,1152]{1,0:T(8,128)(2,1)S(1)} %get-tuple-element.294) | copy-start | bytes 3538948
  436.8 14.8 %copy-start.8 = (f32[1152]{0:T(1024)S(1)}, f32[1152]{0:T(1024)}, u32[]{:S(2)}) copy-start(f32[1152]{0:T(1024)} %get-tuple-element.217) | copy-start | bytes 13828
  451.6 7.1 copy-start.21
  453.0 77.9 %all-gather.27.cloned.1.call-start = ((), (), s32[]{:S(2)}) async-start(), calls=%async_computation.5 | async-start | bytes 4456448 | tf_op jit(solution)/shard_map/all_gather | solution.py:120
  548.1 8.8 %copy-start.13 = (bf16[8192,1,256]{2,0,1:T(8,128)(2,1)S(1)}, bf16[8192,1,256]{2,0,1:T(8,128)(2,1)}, u32[]{:S(2)}) copy-start(bf16[8192,1,256]{2,0,1:T(8,128)(2,1)} %get-tuple-element.525) | copy-start | bytes 12582916 | tf_op jit(solution)/shard_map/while
  586.0 8.8 %copy-start.13 = (bf16[8192,1,256]{2,0,1:T(8,128)(2,1)S(1)}, bf16[8192,1,256]{2,0,1:T(8,128)(2,1)}, u32[]{:S(2)}) copy-start(bf16[8192,1,256]{2,0,1:T(8,128)(2,1)} %get-tuple-element.525) | copy-start | bytes 12582916 | tf_op jit(solution)/shard_map/while
  623.9 8.8 %copy-start.13 = (bf16[8192,1,256]{2,0,1:T(8,128)(2,1)S(1)}, bf16[8192,1,256]{2,0,1:T(8,128)(2,1)}, u32[]{:S(2)}) copy-start(bf16[8192,1,256]{2,0,1:T(8,128)(2,1)} %get-tuple-element.525) | copy-start | bytes 12582916 | tf_op jit(solution)/shard_map/while
  661.7 8.8 %copy-start.13 = (bf16[8192,1,256]{2,0,1:T(8,128)(2,1)S(1)}, bf16[8192,1,256]{2,0,1:T(8,128)(2,1)}, u32[]{:S(2)}) copy-start(bf16[8192,1,256]{2,0,1:T(8,128)(2,1)} %get-tuple-element.525) | copy-start | bytes 12582916 | tf_op jit(solution)/shard_map/while
  (10 other events, 33.3 us)
Sparse Core Ops, SparseCore 0:
  9.0 46.3 all-gather.16
  57.0 36.4 all-gather.20
  95.1 42.1 all-gather.22
  138.8 36.8 all-gather.18
  177.2 36.8 all-gather.24
  215.6 36.9 all-gather.28
  453.1 39.2 all-gather.30
  494.0 36.8 all-gather.26
where the time goes:
time: 740 us; the launch traced here: 736 us
  matrix products  453 us (61%)
  waiting for transfers between devices  148 us (20%)
  other arithmetic  88.5 us (12%)
  between operations  14.4 us (2%)
  starting transfers between devices  13.6 us (2%)
  local copies, waits for them, and re-layouts  13.1 us (2%)
    all_gather x2, waiting for transfers between devices, device_step(): all_k = lax.all_gather(new_k, 'ctx', axis=0, tiled=True)  76.9 us
    dot_general x8, matrix products, one_block(): jnp.einsum('hgqk,khd->qhgd', cache_probs.astype(jnp.bfloat16), cache_v, p...  74.9 us
    dot_general x8, matrix products, one_block(): jnp.einsum('qhgd,khd->hgqk', q_rows, cache_k, preferred_element_type=jnp....  74.6 us
    dot_general x4, matrix products, mlp_block(): jnp.dot(act_bf16, w_down, preferred_element_type=jnp.float32)  70.5 us
    reduce_sum x8, other arithmetic, one_block(): row_sum = cache_probs.sum(axis=-1) + new_probs.sum(axis=-1)  70 us
    all_gather x2, waiting for transfers between devices, device_step(): all_v = lax.all_gather(new_v, 'ctx', axis=0, tiled=True)  69.2 us
    dot_general x4, matrix products, mlp_block(): gate_pre = jnp.dot(normed, w_gate, preferred_element_type=jnp.float32)  65.7 us
    dot_general x3, matrix products, mlp_block(): up_pre = jnp.dot(normed, w_up, preferred_element_type=jnp.float32)  53 us
  transfers between devices with their start and end apart: 12, of which 5 were waited for; matrix products, arithmetic and copies ran while one was open for 49% of the time, Pallas kernels for 0%

commit v1 on v0

v1 whole, which is shorter than its diff:
```python
import functools
import jax
import jax.numpy as jnp
from jax import lax
from jax.sharding import PartitionSpec as P
from jax.experimental import pallas as pl
from jax.experimental.pallas import tpu as pltpu

NORM_EPS = 1e-6
LOG2E = 1.4426950408889634
NEG = -1e30
BF = 768
NS = 3


def rms_rows(x, gain):
    xf = x.astype(jnp.float32)
    inv = lax.rsqrt(jnp.mean(xf * xf, axis=-1, keepdims=True) + NORM_EPS)
    return (xf * inv * gain.astype(jnp.float32)).astype(jnp.bfloat16)


def dotf(a, b):
    return jnp.dot(a, b, preferred_element_type=jnp.float32)


def dot_t(a, b):
    return lax.dot_general(a, b, (((1,), (1,)), ((), ())), preferred_element_type=jnp.float32)


def dense_call(stages, x, weights, q=None, k=None, v=None, halo_k=None, halo_v=None, attn=None, heads=4, name="dense"):
    g_attn, g_mlp, w_q, w_k, w_v, w_o, w_gate, w_up, w_down = weights
    rows, width = x.shape
    ff = w_gate.shape[-1]
    qw = w_q.shape[-1]
    kw = w_k.shape[-1]
    nb = ff // BF
    names = [s for s, _ in stages]
    has_l = "lattn" in names
    mlps = [l for s, l in stages if s == "mlp"]
    qkvs = [l for s, l in stages if s == "qkv"]
    oprojs = [l for s, l in stages if s == "oproj"]
    scale = kw ** -0.5 * LOG2E

    ins = [x, g_attn, g_mlp]
    vm = pl.BlockSpec(memory_space=pltpu.VMEM)
    hb = pl.BlockSpec(memory_space=pl.ANY)
    specs = [vm] * 3
    if has_l:
        ins += [q, k, v, halo_k, halo_v]
        specs += [vm] * 5
    elif attn is not None:
        ins += [attn]
        specs += [vm]
    n_small = len(ins)
    ins += [w_q, w_k, w_v, w_o, w_gate, w_up, w_down]
    specs += [hb] * 7
    outs = [jax.ShapeDtypeStruct((rows, width), jnp.bfloat16)]
    if qkvs:
        outs += [jax.ShapeDtypeStruct((rows, qw), jnp.bfloat16), jax.ShapeDtypeStruct((rows, kw), jnp.bfloat16), jax.ShapeDtypeStruct((rows, kw), jnp.bfloat16)]
    scratch = dict(
        xs=pltpu.VMEM((rows, width), jnp.bfloat16),
        hs=pltpu.VMEM((rows, width), jnp.bfloat16),
        acc=pltpu.VMEM((rows, width), jnp.float32),
        os=pltpu.VMEM((rows, qw), jnp.bfloat16),
        wqb=pltpu.VMEM((width, qw), jnp.bfloat16),
        wkb=pltpu.VMEM((width, kw), jnp.bfloat16),
        wvb=pltpu.VMEM((width, kw), jnp.bfloat16),
        wob=pltpu.VMEM((qw, width), jnp.bfloat16),
        wgb=pltpu.VMEM((NS, width, BF), jnp.bfloat16),
        wub=pltpu.VMEM((NS, width, BF), jnp.bfloat16),
        wdb=pltpu.VMEM((NS, BF, width), jnp.bfloat16),
        msem=pltpu.SemaphoreType.DMA((3, NS)),
        psem=pltpu.SemaphoreType.DMA((4,)),
    )
    if has_l:
        scratch.update(kx=pltpu.VMEM((2 * rows, kw), jnp.bfloat16), vx=pltpu.VMEM((2 * rows, kw), jnp.bfloat16))
    keys = list(scratch)

    def kernel(*refs):
        x_ref, ga_ref, gm_ref = refs[:3]
        if has_l:
            q_ref, k_ref, v_ref, hk_ref, hv_ref = refs[3:8]
        elif attn is not None:
            a_ref = refs[3]
        wq_h, wk_h, wv_h, wo_h, wg_h, wu_h, wd_h = refs[n_small:n_small + 7]
        o_refs = refs[n_small + 7:n_small + 7 + len(outs)]
        sc = dict(zip(keys, refs[n_small + 7 + len(outs):]))
        xs, hs, acc, os_ = sc["xs"], sc["hs"], sc["acc"], sc["os"]

        def wcopies(l, j, slot):
            off = pl.multiple_of(j * BF, BF)
            return [
                pltpu.make_async_copy(wg_h.at[l, :, pl.ds(off, BF)], sc["wgb"].at[slot], sc["msem"].at[0, slot]),
                pltpu.make_async_copy(wu_h.at[l, :, pl.ds(off, BF)], sc["wub"].at[slot], sc["msem"].at[1, slot]),
                pltpu.make_async_copy(wd_h.at[l, pl.ds(off, BF), :], sc["wdb"].at[slot], sc["msem"].at[2, slot]),
            ]

        def start_mlp(l):
            for j in range(NS - 1):
                for c in wcopies(l, j, j):
                    c.start()

        def qkv_copies(l):
            return [pltpu.make_async_copy(src.at[l], sc[dst], sc["psem"].at[i]) for i, (src, dst) in enumerate([(wq_h, "wqb"), (wk_h, "wkb"), (wv_h, "wvb")])]

        def o_copy(l):
            return pltpu.make_async_copy(wo_h.at[l], sc["wob"], sc["psem"].at[3])

        if oprojs:
            o_copy(oprojs[0]).start()
        if stages[0][0] == "qkv":
            for c in qkv_copies(qkvs[0]):
                c.start()
        if mlps:
            start_mlp(mlps[0])
        if qkvs and stages[0][0] != "qkv":
            for c in qkv_copies(qkvs[0]):
                c.start()
        if "oproj" not in names and "mlp" not in names:
            xs_src = x_ref
        else:
            xs_src = None
        cur = [x_ref]

        def do_lattn(l):
            half = rows // 2
            sc["kx"][0:rows, :] = hk_ref[...]
            sc["kx"][rows:2 * rows, :] = k_ref[...]
            sc["vx"][0:rows, :] = hv_ref[...]
            sc["vx"][rows:2 * rows, :] = v_ref[...]
            span = rows + half
            ri = lax.broadcasted_iota(jnp.int32, (half, span), 0)
            ci = lax.broadcasted_iota(jnp.int32, (half, span), 1)
            ok = (ci > ri) & (ci <= ri + rows)
            for t in range(2):
                for h in range(heads):
                    qt = q_ref[t * half:(t + 1) * half, h * kw:(h + 1) * kw]
                    s = dot_t(qt, sc["kx"][t * half:t * half + span, :])
                    s = jnp.where(ok, s, NEG)
                    m = jnp.max(s, axis=1, keepdims=True)
                    p = jnp.exp2((s - m) * scale)
                    den = jnp.sum(p, axis=1, keepdims=True)
                    num = dotf(p.astype(jnp.bfloat16), sc["vx"][t * half:t * half + span, :])
                    os_[t * half:(t + 1) * half, h * kw:(h + 1) * kw] = (num / den).astype(jnp.bfloat16)

        def do_oproj(l):
            src = os_ if has_l else a_ref
            o_copy(l).wait()
            xs[...] = (cur[0][...].astype(jnp.float32) + dotf(src[...], sc["wob"][...])).astype(jnp.bfloat16)
            cur[0] = xs

        def do_mlp(l):
            hs[...] = rms_rows(cur[0][...], gm_ref[l:l + 1, :])
            acc[...] = cur[0][...].astype(jnp.float32)

            def step(j, slot, nxt_slot):
                for c in wcopies(l, j, slot):
                    c.wait()

                @pl.when(j + NS - 1 < nb)
                def _():
                    for c in wcopies(l, j + NS - 1, nxt_slot):
                        c.start()
                ga = dotf(hs[...], sc["wgb"][slot])
                up = dotf(hs[...], sc["wub"][slot])
                a = (jax.nn.gelu(ga, approximate=True) * up).astype(jnp.bfloat16)
                acc[...] += dotf(a, sc["wdb"][slot])

            def loop(jj, _):
                for s in range(NS):
                    step(jj * NS + s, s, (s + NS - 1) % NS)
                return 0
            lax.fori_loop(0, nb // NS, loop, 0)
            xs[...] = acc[...].astype(jnp.bfloat16)
            cur[0] = xs

        def do_qkv(l):
            hs[...] = rms_rows(cur[0][...], ga_ref[l:l + 1, :])
            for c in qkv_copies(l):
                c.wait()
            o_refs[2][...] = dotf(hs[...], sc["wkb"][...]).astype(jnp.bfloat16)
            o_refs[3][...] = dotf(hs[...], sc["wvb"][...]).astype(jnp.bfloat16)
            o_refs[1][...] = dotf(hs[...], sc["wqb"][...]).astype(jnp.bfloat16)

        for s, l in stages:
            dict(lattn=do_lattn, oproj=do_oproj, mlp=do_mlp, qkv=do_qkv)[s](l)
        o_refs[0][...] = cur[0][...]

    flops = 0
    for s, l in stages:
        flops += 2 * rows * width * {"mlp": 3 * ff, "qkv": qw + 2 * kw, "oproj": qw, "lattn": 4 * rows}[s]
    return pl.pallas_call(
        kernel, out_shape=tuple(outs), in_specs=specs, out_specs=tuple([vm] * len(outs)),
        scratch_shapes=list(scratch.values()),
        cost_estimate=pl.CostEstimate(flops=flops, bytes_accessed=len(mlps) * 3 * width * ff * 2 + 10**6, transcendentals=0),
        compiler_params=pltpu.CompilerParams(vmem_limit_bytes=60 * 1024 * 1024), name=name)(*ins)


MESH = pl.DeviceIdType.MESH
CB = 1024


def flash_units(q_ref, m_ref, l_ref, acc_ref, s_scr, k_of, v_of, keys, mask, heads, dim, scale):
    def scores(h):
        return dot_t(q_ref[:, h * dim:(h + 1) * dim], k_of())
    s_scr[0, :, 0:keys] = scores(0)
    for h in range(heads):
        if h + 1 < heads:
            s_scr[(h + 1) % 2, :, 0:keys] = scores(h + 1)
        s = s_scr[h % 2, :, 0:keys]
        if mask is not None:
            s = jnp.where(mask, s, -jnp.inf)
        m_prev = m_ref[h]
        mx = s[:, 0:128]
        for c in range(1, keys // 128):
            mx = jnp.maximum(mx, s[:, c * 128:(c + 1) * 128])
        m_cur = jnp.maximum(m_prev, jnp.max(mx, axis=1, keepdims=True))
        alpha = jnp.exp2((m_prev - m_cur) * scale)
        lsum = alpha * l_ref[h]
        parts = []
        for c in range(keys // 128):
            e = jnp.exp2((s[:, c * 128:(c + 1) * 128] - m_cur) * scale)
            lsum = lsum + e
            parts.append(e.astype(jnp.bfloat16))
        l_ref[h] = lsum
        m_ref[h] = m_cur
        pv = dotf(jnp.concatenate(parts, axis=1), v_of())
        for c in range(dim // 128):
            lo = h * dim + c * 128
            acc_ref[:, lo:lo + 128] = acc_ref[:, lo:lo + 128] * alpha + pv[:, c * 128:(c + 1) * 128]


def global_call(q, k, v, ck, cv, clen, n_ctx, heads=4):
    rows, qw = q.shape
    dim = k.shape[1]
    slots = ck.shape[0]
    ncb = slots // CB
    n_chip = n_ctx // 2
    scale = dim ** -0.5 * LOG2E
    n_arr = 2 * (n_chip - 1)

    def kernel(clen_ref, q_ref, k_ref, v_ref, ck_h, cv_h, o_ref, kv, m_ref, l_ref, acc_ref, s_scr, cb, csem, rs, rr, ps, pr):
        me = lax.axis_index("ctx")
        z, p = me // 2, me % 2
        step_dir = 1 - 2 * p
        partner = z * 2 + (1 - p)
        succ = ((z + step_dir + n_chip) % n_chip) * 2 + p
        pred = ((z - step_dir + n_chip) % n_chip) * 2 + p

        def mine(s):
            return ((z - step_dir * s + n_chip) % n_chip) * 2 + p

        def theirs(s):
            return ((z + step_dir * s + n_chip) % n_chip) * 2 + (1 - p)

        barrier = pltpu.get_barrier_semaphore()
        for who in (pred, partner):
            pl.semaphore_signal(barrier, inc=1, device_id={"ctx": who}, device_id_type=MESH)
        pl.semaphore_wait(barrier, 2)

        own = (k_ref, v_ref)

        def own_send(t, who, ss, rsem, i):
            return pltpu.make_async_remote_copy(src_ref=own[t], dst_ref=kv.at[t, me], send_sem=ss.at[i], recv_sem=rsem.at[i], device_id={"ctx": who}, device_id_type=MESH)

        def fwd(a, who, ss, rsem, i):
            d = mine(a // 2 + 1)
            return pltpu.make_async_remote_copy(src_ref=kv.at[a % 2, d], dst_ref=kv.at[a % 2, d], send_sem=ss.at[i], recv_sem=rsem.at[i], device_id={"ctx": who}, device_id_type=MESH)

        for t in range(2):
            own_send(t, succ, rs, rr, t).start()
        for t in range(2):
            own_send(t, partner, ps, pr, t).start()

        def wait_arrival(a):
            d = mine(a // 2 + 1)
            pltpu.make_async_remote_copy(src_ref=kv.at[a % 2, d], dst_ref=kv.at[a % 2, d], send_sem=rs.at[a], recv_sem=rr.at[a], device_id={"ctx": pred}, device_id_type=MESH).wait_recv()

        def wait_partner(t, s):
            d = theirs(s)
            pltpu.make_async_remote_copy(src_ref=kv.at[t, d], dst_ref=kv.at[t, d], send_sem=ps.at[2 * s + t], recv_sem=pr.at[2 * s + t], device_id={"ctx": partner}, device_id_type=MESH).wait_recv()

        def handle(a):
            wait_arrival(a)

            @pl.when(a + 2 < n_arr)
            def _():
                fwd(a, succ, rs, rr, a + 2).start()
            fwd(a, partner, ps, pr, a + 2).start()

        def ccopy(i):
            off = pl.multiple_of(i * CB, CB)
            return [pltpu.make_async_copy(src.at[pl.ds(off, CB), :], cb.at[t, i % 2], csem.at[t, i % 2]) for t, src in ((0, ck_h), (1, cv_h))]

        for c in ccopy(0):
            c.start()
        m_ref[...] = jnp.full_like(m_ref, -jnp.inf)
        l_ref[...] = jnp.zeros_like(l_ref)
        acc_ref[...] = jnp.zeros_like(acc_ref)
        units = functools.partial(flash_units, q_ref, m_ref, l_ref, acc_ref, s_scr, heads=heads, dim=dim, scale=scale)
        ri = lax.broadcasted_iota(jnp.int32, (rows, rows), 0)
        ci = lax.broadcasted_iota(jnp.int32, (rows, rows), 1)
        units(lambda: k_ref[...], lambda: v_ref[...], rows, ci <= ri)

        def cache_step(masked):
            def body(i, carry):
                for c in ccopy(i):
                    c.wait()

                @pl.when(i + 1 < ncb)
                def _():
                    for c in ccopy(i + 1):
                        c.start()

                @pl.when(i >= 1)
                def _():
                    handle(i - 1)
                mask = None
                if masked:
                    mask = (lax.broadcasted_iota(jnp.int32, (1, CB), 1) + i * CB) < clen_ref[0]
                units(lambda: cb[0, i % 2], lambda: cb[1, i % 2], CB, mask)
                return carry
            return body
        lax.fori_loop(0, ncb // 2, cache_step(False), 0)
        lax.fori_loop(ncb // 2, ncb, cache_step(True), 0)

        def shard(d):
            @pl.when(d < me)
            def _():
                units(lambda: kv[0, d], lambda: kv[1, d], rows, None)

        wait_partner(0, 0)
        wait_partner(1, 0)
        shard(partner)

        def new_step(s, carry):
            @pl.when(s + ncb - 2 < n_arr)
            def _():
                handle(s + ncb - 2)
            shard(mine(s))
            wait_partner(0, s)
            wait_partner(1, s)
            shard(theirs(s))
            return carry
        lax.fori_loop(1, n_chip, new_step, 0)

        for t in range(2):
            own_send(t, succ, rs, rr, t).wait_send()
            own_send(t, partner, ps, pr, t).wait_send()

        def drain(a, carry):
            @pl.when(a + 2 < n_arr)
            def _():
                fwd(a, succ, rs, rr, a + 2).wait_send()
            fwd(a, partner, ps, pr, a + 2).wait_send()
            return carry
        lax.fori_loop(0, n_arr, drain, 0)
        for h in range(heads):
            den = jnp.sum(l_ref[h], axis=1, keepdims=True)
            o_ref[:, h * dim:(h + 1) * dim] = (acc_ref[:, h * dim:(h + 1) * dim] / den).astype(jnp.bfloat16)

    vm = pl.BlockSpec(memory_space=pltpu.VMEM)
    hb = pl.BlockSpec(memory_space=pl.ANY)
    sem = pltpu.SemaphoreType.DMA
    return pl.pallas_call(
        kernel, out_shape=jax.ShapeDtypeStruct((rows, qw), jnp.bfloat16),
        in_specs=[pl.BlockSpec(memory_space=pltpu.SMEM), vm, vm, vm, hb, hb], out_specs=vm,
        scratch_shapes=[
            pltpu.VMEM((2, n_ctx, rows, dim), jnp.bfloat16),
            pltpu.VMEM((heads, rows, 128), jnp.float32), pltpu.VMEM((heads, rows, 128), jnp.float32),
            pltpu.VMEM((rows, qw), jnp.float32), pltpu.VMEM((2, rows, CB), jnp.float32),
            pltpu.VMEM((2, 2, CB, dim), jnp.bfloat16), sem((2, 2)),
            sem((n_arr,)), sem((n_arr,)), sem((n_arr + 2,)), sem((n_arr + 2,))],
        cost_estimate=pl.CostEstimate(flops=4 * rows * qw * (slots + n_ctx * rows), bytes_accessed=4 * slots * dim, transcendentals=0),
        compiler_params=pltpu.CompilerParams(vmem_limit_bytes=60 * 1024 * 1024, collective_id=1, has_side_effects=True), name="gattn")(clen, q, k, v, ck, cv)


def solution(mesh):
    n_ctx = mesh.shape['ctx']
    shift_pairs = [(i, i + 1) for i in range(n_ctx - 1)]
    row_spec = P(('dp', 'ctx'), None)
    cache_spec = P(None, ('dp', 'ctx'), None, None)
    local_spec = P(None, 'dp', None, None)
    in_specs = (row_spec, P('dp'), cache_spec, cache_spec, local_spec, local_spec) + (P(),) * 9

    def device_step(x, cache_len, k_cache, v_cache, k_local, v_local, g_attn, g_mlp, w_q, w_k, w_v, w_o, w_gate, w_up, w_down):
        weights = (g_attn, g_mlp, w_q, w_k, w_v, w_o, w_gate, w_up, w_down)
        is_first = lax.axis_index('ctx') == 0
        n_pairs = k_cache.shape[0]
        caches = [[lax.all_gather(c[i, :, 0, :], 'ctx', axis=0, tiled=True) for c in (k_cache, v_cache)] for i in range(n_pairs)]
        _, q, k, v = dense_call([("qkv", 0)], x, weights, name="qkv")
        for i in range(n_pairs):
            halo_k = jnp.where(is_first, k_local[i, :, 0, :], lax.ppermute(k, 'ctx', shift_pairs))
            halo_v = jnp.where(is_first, v_local[i, :, 0, :], lax.ppermute(v, 'ctx', shift_pairs))
            l = 2 * i
            x, q, k, v = dense_call([("lattn", l), ("oproj", l), ("mlp", l), ("qkv", l + 1)], x, weights, q=q, k=k, v=v, halo_k=halo_k, halo_v=halo_v, name="local%d" % i)
            o = global_call(q, k, v, caches[i][0], caches[i][1], cache_len, n_ctx)
            last = i == n_pairs - 1
            r = dense_call([("oproj", l + 1), ("mlp", l + 1)] + ([] if last else [("qkv", l + 2)]), x, weights, attn=o, name="glob%d" % i)
            x = r[0]
            if not last:
                q, k, v = r[1:]
        return x

    return jax.shard_map(device_step, mesh=mesh, in_specs=in_specs, out_specs=row_spec, check_vma=False)
```

time: 740 us -> 391 us (0.53)
  matrix products: 453 us -> 0 us
  Pallas kernels: 0 us -> 323 us
  waiting for transfers between devices: 148 us -> 27 us
  other arithmetic: 88.5 us -> 2.99 us
  local copies, waits for them, and re-layouts: 13.1 us -> 3.79 us
    dot_general x67 -> x0, matrix products: 453 us -> none  [the longest x8 74.9 us: one_block(): jnp.einsum('hgqk,khd->qhgd', cache_probs.astype(jnp.bfloat16), cache_v, p...]
    pallas_call x0 -> x7, Pallas kernels: none -> 323 us  [the longest x5 179 us: dense_call(): pl.pallas_call(kernel, out_shape=tuple(outs), in_specs=specs, out_specs=t...]
    all_gather x8 -> x4, waiting for transfers between devices: 146 us -> 12.8 us  [device_step(): lax.all_gather(c[i, :, 0, :], 'ctx', axis=0, tiled=True)]
    reduce_sum x11 -> x0, other arithmetic: 75.4 us -> none  [the longest x8 70 us: one_block(): row_sum = cache_probs.sum(axis=-1) + new_probs.sum(axis=-1)]
    ppermute x4, waiting for transfers between devices: 0.11 us -> 13.4 us  [the longest x2 9.72 us: device_step(): lax.ppermute(v, 'ctx', shift_pairs)]
  transfers between devices with their start and end apart: 12 -> 8, of which waited for: 5 -> 5; matrix products, arithmetic and copies ran while one was open for 49% -> 1% of each run, Pallas kernels for 0% -> 59%
where the time goes in v1:
time: 391 us; the launch traced here: 385 us
  Pallas kernels  323 us (83%)
  waiting for transfers between devices  27 us (7%)
  between operations  14.2 us (4%)
  starting transfers between devices  13.6 us (3%)
    pallas_call x5, Pallas kernels, dense_call(): pl.pallas_call(kernel, out_shape=tuple(outs), in_specs=specs, out_specs=t...  179 us
    pallas_call x2, Pallas kernels, global_call(): pl.pallas_call(kernel, out_shape=jax.ShapeDtypeStruct((rows, qw), jnp.bfl...  144 us
    all_gather x4, waiting for transfers between devices, device_step(): lax.all_gather(c[i, :, 0, :], 'ctx', axis=0, tiled=True)  12.8 us
    ppermute x2, waiting for transfers between devices, device_step(): lax.ppermute(v, 'ctx', shift_pairs)  9.72 us
    ppermute x2, starting transfers between devices, device_step(): lax.ppermute(k, 'ctx', shift_pairs)  9.34 us
  transfers between devices with their start and end apart: 8, of which 5 were waited for; matrix products, arithmetic and copies ran while one was open for 1% of the time, Pallas kernels for 59%

profile of v1, /device:TPU:21, one launch (start us, length us, event | category | flops | bytes accessed | tf_op | source)
XLA Modules:
  0.0 384.8 jit_solution(8379167787489647227)
XLA Ops:
  6.6 1.9 fusion.1
  8.4 0.1 all-gather.9.cloned.1.call-update
  8.5 0.1 all-gather.11.cloned.1.call-start
  8.6 1.9 fusion
  10.4 0.1 all-gather.11.cloned.1.call-update
  10.5 0.1 all-gather.13.cloned.1.call-start
  10.6 0.7 all-gather.13.cloned.1.call-update
  11.3 0.1 all-gather.15.cloned.1.call-start
  11.4 7.1 %qkv.1 = (bf16[512,1152]{1,0:T(8,128)(2,1)}, bf16[512,1024]{1,0:T(8,128)(2,1)}, bf16[512,256]{1,0:T(8,128)(2,1)}, bf16[512,256]{1,0:T(8,128)(2,1)}) custom-call(bf16[512,1152]{1,0:T(8,128)(2,1)} %refs_0_.3, bf16[4,1152]{1,0:T(4,128)(2,1)} %refs_1_.9, bf16[4,1152]{1,0:T(4,128)(2,1)} %refs_2_.9, bf16[4,1152,1024]{2,1,0:T(8,128)(2,1)} %refs_4_.5, ...), custom_call_target="tpu_custom_call" | custom-call | flops 1811939328 | bytes 1000000 | tf_op jit(solution)/shard_map/qkv/pallas_call | solution.py:192
  18.5 5.1 %collective-permute-start = (bf16[512,256]{1,0:T(8,128)(2,1)}, bf16[512,256]{1,0:T(8,128)(2,1)S(1)}, u32[]{:S(2)}, u32[]{:S(2)}) collective-permute-start(bf16[512,256]{1,0:T(8,128)(2,1)} %get-tuple-element.21.refs_4_), channel_id=1, source_target_pairs={{0,1},{1,2},{2,3},{3,4},{4,5},{5,6},{6,7},{7,8},{8,9},{9,10},{10,1... | collective-permute-start | bytes 786440 | tf_op jit(solution)/shard_map/ppermute | solution.py:393
  23.6 2.0 collective-permute-start.1
  25.5 0.1 all-gather.15.cloned.1.call-update
  26.3 2.5 collective-permute-done
  28.8 0.7 bitcast_select_fusion.3.refs_6_
  29.5 7.7 %collective-permute-done.1 = bf16[512,256]{1,0:T(8,128)(2,1)S(1)} collective-permute-done((bf16[512,256]{1,0:T(8,128)(2,1)}, bf16[512,256]{1,0:T(8,128)(2,1)S(1)}, u32[]{:S(2)}, u32[]{:S(2)}) %collective-permute-start.1) | collective-permute-done | bytes 262176 | tf_op jit(solution)/shard_map/ppermute | solution.py:394
  37.2 0.7 bitcast_select_fusion.2.refs_7_
  37.9 43.7 %local0.1 = (bf16[512,1152]{1,0:T(8,128)(2,1)}, bf16[512,1024]{1,0:T(8,128)(2,1)}, bf16[512,256]{1,0:T(8,128)(2,1)}, bf16[512,256]{1,0:T(8,128)(2,1)}) custom-call(bf16[512,1152]{1,0:T(8,128)(2,1)} %refs_0_.3, bf16[4,1152]{1,0:T(4,128)(2,1)} %refs_1_.9, bf16[4,1152]{1,0:T(4,128)(2,1)} %refs_2_.9, bf16[512,1024]{1,0:T(8,128)(2,1)} %get-tuple-element.20.refs_3_, ...), custom_call_target="tpu_custom_call" | custom-call | flops 29896998912 | bytes 48775744 | tf_op jit(solution)/shard_map/local0/pallas_call | solution.py:192
  81.7 0.0 all-gather.9.cloned.1.call-done
  81.7 12.7 %all-gather.11.cloned.1.call-done = bf16[1,8192,1,256]{3,1,2,0:T(8,128)(2,1)} async-done(((bf16[1,512,1,256]{3,1,2,0:T(8,128)(2,1)}), bf16[1,8192,1,256]{3,1,2,0:T(8,128)(2,1)}) %all-gather.11.cloned.1.call-update) | async-done | bytes 4194320 | tf_op jit(solution)/shard_map/all_gather | solution.py:390
  94.4 88.8 %gattn.2.refs_3_ = bf16[512,1024]{1,0:T(8,128)(2,1)} custom-call(s32[1]{0:T(128)S(6)} %copy.16.clen_ref, bf16[512,1024]{1,0:T(8,128)(2,1)} %get-tuple-element.24.q_ref, bf16[512,256]{1,0:T(8,128)(2,1)} %get-tuple-element.25.k_ref, bf16[512,256]{1,0:T(8,128)(2,1)} %get-tuple-element.26.v_ref, bf16[8192,256]{1,0:T(8,128)(2,1)} %bitcast.14, ...), custom_call_target="tpu_custom_call" | custom-call | flops 34359738368 | bytes 8388608 | tf_op jit(solution)/shard_map/gattn/pallas_call | solution.py:365
  183.3 43.4 %glob0.1 = (bf16[512,1152]{1,0:T(8,128)(2,1)}, bf16[512,1024]{1,0:T(8,128)(2,1)}, bf16[512,256]{1,0:T(8,128)(2,1)}, bf16[512,256]{1,0:T(8,128)(2,1)}) custom-call(bf16[512,1152]{1,0:T(8,128)(2,1)} %get-tuple-element.23.refs_0_, bf16[4,1152]{1,0:T(4,128)(2,1)} %refs_1_.9, bf16[4,1152]{1,0:T(4,128)(2,1)} %refs_2_.9, bf16[512,1024]{1,0:T(8,128)(2,1)} %gattn.2.refs_3_, ...), custom_call_target="tpu_custom_call" | custom-call | flops 27481079808 | bytes 48775744 | tf_op jit(solution)/shard_map/glob0/pallas_call | solution.py:192
  226.7 4.2 %collective-permute-start.2 = (bf16[512,256]{1,0:T(8,128)(2,1)}, bf16[512,256]{1,0:T(8,128)(2,1)S(1)}, u32[]{:S(2)}, u32[]{:S(2)}) collective-permute-start(bf16[512,256]{1,0:T(8,128)(2,1)} %get-tuple-element.29.refs_4_), channel_id=1, source_target_pairs={{0,1},{1,2},{2,3},{3,4},{4,5},{5,6},{6,7},{7,8},{8,9},{9,10},{10,1... | collective-permute-start | bytes 786440 | tf_op jit(solution)/shard_map/ppermute | solution.py:393
  231.0 2.1 collective-permute-start.3
  233.1 1.1 collective-permute-done.2
  234.2 0.8 bitcast_select_fusion.1.refs_6_
  235.0 2.0 collective-permute-done.3
  237.1 0.7 bitcast_select_fusion.refs_7_
  237.8 43.3 %local1.1 = (bf16[512,1152]{1,0:T(8,128)(2,1)}, bf16[512,1024]{1,0:T(8,128)(2,1)}, bf16[512,256]{1,0:T(8,128)(2,1)}, bf16[512,256]{1,0:T(8,128)(2,1)}) custom-call(bf16[512,1152]{1,0:T(8,128)(2,1)} %get-tuple-element.27.refs_0_, bf16[4,1152]{1,0:T(4,128)(2,1)} %refs_1_.9, bf16[4,1152]{1,0:T(4,128)(2,1)} %refs_2_.9, ...), custom_call_target="tpu_custom_call" | custom-call | flops 29896998912 | bytes 48775744 | tf_op jit(solution)/shard_map/local1/pallas_call | solution.py:192
  281.1 0.0 all-gather.13.cloned.1.call-done
  281.2 0.0 all-gather.15.cloned.1.call-done
  281.2 55.3 %gattn.3.refs_3_ = bf16[512,1024]{1,0:T(8,128)(2,1)} custom-call(s32[1]{0:T(128)S(6)} %copy.16.clen_ref, bf16[512,1024]{1,0:T(8,128)(2,1)} %get-tuple-element.32.q_ref, bf16[512,256]{1,0:T(8,128)(2,1)} %get-tuple-element.33.k_ref, bf16[512,256]{1,0:T(8,128)(2,1)} %get-tuple-element.34.v_ref, bf16[8192,256]{1,0:T(8,128)(2,1)} %bitcast.12, ...), custom_call_target="tpu_custom_call" | custom-call | flops 34359738368 | bytes 8388608 | tf_op jit(solution)/shard_map/gattn/pallas_call | solution.py:365
  336.5 41.5 %glob1.1 = bf16[512,1152]{1,0:T(8,128)(2,1)} custom-call(bf16[512,1152]{1,0:T(8,128)(2,1)} %get-tuple-element.31.refs_0_, bf16[4,1152]{1,0:T(4,128)(2,1)} %refs_1_.9, bf16[4,1152]{1,0:T(4,128)(2,1)} %refs_2_.9, bf16[512,1024]{1,0:T(8,128)(2,1)} %gattn.3.refs_3_, bf16[4,1152,1024]{2,1,0:T(8,128)(2,1)} %refs_4_.5, bf16[4,1152,256]{2,1,0:T(8,128)(2,1)} %refs_5_.5, ...), custom_call_target="tpu_custom_call" | custom-call | flops 25669140480 | bytes 48775744 | tf_op jit(solution)/shard_map/glob1/pallas_call | solution.py:192
  (9 shorter events, 0.0 us)
Async XLA Ops:
  6.5 75.2 %all-gather.9.cloned.1.call-start = ((), (), s32[]{:S(2)}) async-start(), calls=%async_computation | async-start | bytes 4456448 | tf_op jit(solution)/shard_map/all_gather | solution.py:390
  8.5 85.9 %all-gather.11.cloned.1.call-start = ((), (), s32[]{:S(2)}) async-start(), calls=%async_computation.1 | async-start | bytes 4456448 | tf_op jit(solution)/shard_map/all_gather | solution.py:390
  10.5 270.6 %all-gather.13.cloned.1.call-start = ((), (), s32[]{:S(2)}) async-start(), calls=%async_computation.2 | async-start | bytes 4456448 | tf_op jit(solution)/shard_map/all_gather | solution.py:390
  11.3 17.5 %copy-start = (bf16[2,512,1,256]{3,1,2,0:T(8,128)(2,1)S(1)}, bf16[2,512,1,256]{3,1,2,0:T(8,128)(2,1)}, u32[]{:S(2)}) copy-start(bf16[2,512,1,256]{3,1,2,0:T(8,128)(2,1)} %param.19) | copy-start | bytes 1572868
  11.3 25.9 %copy-start.2 = (bf16[2,512,1,256]{3,1,2,0:T(8,128)(2,1)S(1)}, bf16[2,512,1,256]{3,1,2,0:T(8,128)(2,1)}, u32[]{:S(2)}) copy-start(bf16[2,512,1,256]{3,1,2,0:T(8,128)(2,1)} %param.20) | copy-start | bytes 1572868
  11.3 269.8 %all-gather.15.cloned.1.call-start = ((), (), s32[]{:S(2)}) async-start(), calls=%async_computation.3 | async-start | bytes 4456448 | tf_op jit(solution)/shard_map/all_gather | solution.py:390
  18.5 10.3 %collective-permute-start = (bf16[512,256]{1,0:T(8,128)(2,1)}, bf16[512,256]{1,0:T(8,128)(2,1)S(1)}, u32[]{:S(2)}, u32[]{:S(2)}) collective-permute-start(bf16[512,256]{1,0:T(8,128)(2,1)} %get-tuple-element.21.refs_4_), channel_id=1, source_target_pairs={{0,1},{1,2},{2,3},{3,4},{4,5},{5,6},{6,7},{7,8},{8,9},{9,10},{10,1... | collective-permute-start | bytes 786440 | tf_op jit(solution)/shard_map/ppermute | solution.py:393
  23.6 13.6 %collective-permute-start.1 = (bf16[512,256]{1,0:T(8,128)(2,1)}, bf16[512,256]{1,0:T(8,128)(2,1)S(1)}, u32[]{:S(2)}, u32[]{:S(2)}) collective-permute-start(bf16[512,256]{1,0:T(8,128)(2,1)} %get-tuple-element.22.refs_5_), channel_id=1, source_target_pairs={{0,1},{1,2},{2,3},{3,4},{4,5},{5,6},{6,7},{7,8},{8,9},{9,10},{10,1... | collective-permute-start | bytes 786440 | tf_op jit(solution)/shard_map/ppermute | solution.py:394
  183.2 51.0 %copy-start.1 = (bf16[2,512,1,256]{3,1,2,0:T(8,128)(2,1)S(1)}, bf16[2,512,1,256]{3,1,2,0:T(8,128)(2,1)}, u32[]{:S(2)}) copy-start(bf16[2,512,1,256]{3,1,2,0:T(8,128)(2,1)} %param.19) | copy-start | bytes 1572868
  183.3 53.8 %copy-start.3 = (bf16[2,512,1,256]{3,1,2,0:T(8,128)(2,1)S(1)}, bf16[2,512,1,256]{3,1,2,0:T(8,128)(2,1)}, u32[]{:S(2)}) copy-start(bf16[2,512,1,256]{3,1,2,0:T(8,128)(2,1)} %param.20) | copy-start | bytes 1572868
  226.7 7.5 %collective-permute-start.2 = (bf16[512,256]{1,0:T(8,128)(2,1)}, bf16[512,256]{1,0:T(8,128)(2,1)S(1)}, u32[]{:S(2)}, u32[]{:S(2)}) collective-permute-start(bf16[512,256]{1,0:T(8,128)(2,1)} %get-tuple-element.29.refs_4_), channel_id=1, source_target_pairs={{0,1},{1,2},{2,3},{3,4},{4,5},{5,6},{6,7},{7,8},{8,9},{9,10},{10,1... | collective-permute-start | bytes 786440 | tf_op jit(solution)/shard_map/ppermute | solution.py:393
  231.0 6.1 %collective-permute-start.3 = (bf16[512,256]{1,0:T(8,128)(2,1)}, bf16[512,256]{1,0:T(8,128)(2,1)S(1)}, u32[]{:S(2)}, u32[]{:S(2)}) collective-permute-start(bf16[512,256]{1,0:T(8,128)(2,1)} %get-tuple-element.30.refs_5_), channel_id=1, source_target_pairs={{0,1},{1,2},{2,3},{3,4},{4,5},{5,6},{6,7},{7,8},{8,9},{9,10},{10,1... | collective-permute-start | bytes 786440 | tf_op jit(solution)/shard_map/ppermute | solution.py:394
Sparse Core Ops, SparseCore 0:
  9.0 46.7 all-gather.8
  57.4 36.9 all-gather.10
  96.1 41.2 all-gather.12
  138.8 41.6 all-gather.14

commit v2 on v1

--- a/solution.py
+++ b/solution.py
@@ -8,9 +8,9 @@
 
 NORM_EPS = 1e-6
 LOG2E = 1.4426950408889634
-NEG = -1e30
+MESH = pl.DeviceIdType.MESH
 BF = 768
-NS = 3
+NS = 2
 
 
 def rms_rows(x, gain):
@@ -27,7 +27,7 @@
     return lax.dot_general(a, b, (((1,), (1,)), ((), ())), preferred_element_type=jnp.float32)
 
 
-def dense_call(stages, x, weights, q=None, k=None, v=None, halo_k=None, halo_v=None, attn=None, heads=4, name="dense"):
+def dense_call(stages, x, weights, local=None, caches=None, pair=0, attn=None, heads=4, n_ctx=0, cid=None, name="dense"):
     g_attn, g_mlp, w_q, w_k, w_v, w_o, w_gate, w_up, w_down = weights
     rows, width = x.shape
     ff = w_gate.shape[-1]
@@ -38,6 +38,9 @@
     has_l = "lattn" in names
     mlps = [l for s, l in stages if s == "mlp"]
     qkvs = [l for s, l in stages if s == "qkv"]
+    last_qkv = stages[-1][0] == "qkv"
+    n_chip = n_ctx // 2
+    n_arr = 2 * (n_chip - 1)
     oprojs = [l for s, l in stages if s == "oproj"]
     scale = kw ** -0.5 * LOG2E
 
@@ -45,17 +48,20 @@
     vm = pl.BlockSpec(memory_space=pltpu.VMEM)
     hb = pl.BlockSpec(memory_space=pl.ANY)
     specs = [vm] * 3
-    if has_l:
-        ins += [q, k, v, halo_k, halo_v]
-        specs += [vm] * 5
-    elif attn is not None:
+    if attn is not None:
         ins += [attn]
         specs += [vm]
     n_small = len(ins)
     ins += [w_q, w_k, w_v, w_o, w_gate, w_up, w_down]
     specs += [hb] * 7
+    if has_l:
+        ins += list(local) + list(caches)
+        specs += [hb] * 4
+    n_in = len(ins)
     outs = [jax.ShapeDtypeStruct((rows, width), jnp.bfloat16)]
-    if qkvs:
+    out_specs = [vm]
+    if last_qkv:
+        out_specs += [vm] * 3
         outs += [jax.ShapeDtypeStruct((rows, qw), jnp.bfloat16), jax.ShapeDtypeStruct((rows, kw), jnp.bfloat16), jax.ShapeDtypeStruct((rows, kw), jnp.bfloat16)]
     scratch = dict(
         xs=pltpu.VMEM((rows, width), jnp.bfloat16),
@@ -73,19 +79,28 @@
         psem=pltpu.SemaphoreType.DMA((4,)),
     )
     if has_l:
-        scratch.update(kx=pltpu.VMEM((2 * rows, kw), jnp.bfloat16), vx=pltpu.VMEM((2 * rows, kw), jnp.bfloat16))
+        outs += [jax.ShapeDtypeStruct((2, n_ctx * rows, kw), jnp.bfloat16)]
+        out_specs += [hb]
+        scratch.update(
+            kvx=pltpu.VMEM((2, 2 * rows, kw), jnp.bfloat16),
+            qs=pltpu.VMEM((rows, qw), jnp.bfloat16),
+            own=pltpu.VMEM((2, rows, kw), jnp.bfloat16),
+            hsem=pltpu.SemaphoreType.DMA((2, 2)),
+            osem=pltpu.SemaphoreType.DMA((2, 2)),
+            rs=pltpu.SemaphoreType.DMA((n_arr,)), rr=pltpu.SemaphoreType.DMA((n_arr,)),
+            ps=pltpu.SemaphoreType.DMA((n_arr + 2,)), pr=pltpu.SemaphoreType.DMA((n_arr + 2,)),
+        )
     keys = list(scratch)
 
     def kernel(*refs):
         x_ref, ga_ref, gm_ref = refs[:3]
-        if has_l:
-            q_ref, k_ref, v_ref, hk_ref, hv_ref = refs[3:8]
-        elif attn is not None:
+        if attn is not None:
             a_ref = refs[3]
         wq_h, wk_h, wv_h, wo_h, wg_h, wu_h, wd_h = refs[n_small:n_small + 7]
-        o_refs = refs[n_small + 7:n_small + 7 + len(outs)]
-        sc = dict(zip(keys, refs[n_small + 7 + len(outs):]))
+        o_refs = refs[n_in:n_in + len(outs)]
+        sc = dict(zip(keys, refs[n_in + len(outs):]))
         xs, hs, acc, os_ = sc["xs"], sc["hs"], sc["acc"], sc["os"]
+        sent = [0]
 
         def wcopies(l, j, slot):
             off = pl.multiple_of(j * BF, BF)
@@ -106,48 +121,118 @@
         def o_copy(l):
             return pltpu.make_async_copy(wo_h.at[l], sc["wob"], sc["psem"].at[3])
 
-        if oprojs:
+        if attn is not None:
             o_copy(oprojs[0]).start()
-        if stages[0][0] == "qkv":
+        if qkvs:
             for c in qkv_copies(qkvs[0]):
                 c.start()
-        if mlps:
-            start_mlp(mlps[0])
-        if qkvs and stages[0][0] != "qkv":
-            for c in qkv_copies(qkvs[0]):
+        if attn is None:
+            o_copy(oprojs[0]).start()
+        start_mlp(mlps[0])
+        cur = [x_ref]
+
+        if has_l:
+            kl_h, vl_h, kc_h, vc_h = refs[n_small + 7:n_in]
+            cc = o_refs[-1]
+            kvx, qs, own = sc["kvx"], sc["qs"], sc["own"]
+            hsem, osem, rs, rr, ps, pr = (sc[n] for n in ("hsem", "osem", "rs", "rr", "ps", "pr"))
+            me = lax.axis_index("ctx")
+            z, p = me // 2, me % 2
+            way = 1 - 2 * p
+            partner = z * 2 + (1 - p)
+            succ = ((z + way + n_chip) % n_chip) * 2 + p
+            pred = ((z - way + n_chip) % n_chip) * 2 + p
+
+            def block(t, d):
+                return cc.at[t, pl.ds(pl.multiple_of(d * rows, rows), rows), :]
+
+            def mine(a):
+                return ((z - way * (a // 2 + 1) + n_chip) % n_chip) * 2 + p
+
+            def theirs(a):
+                return ((z + way * (a // 2) + n_chip) % n_chip) * 2 + (1 - p)
+
+            def remote(src, dst, ssem, rsem, who):
+                return pltpu.make_async_remote_copy(src_ref=src, dst_ref=dst, send_sem=ssem, recv_sem=rsem, device_id={"ctx": who}, device_id_type=MESH)
+
+            own_in = [pltpu.make_async_copy(src.at[pair], own.at[t], osem.at[0, t]) for t, src in ((0, kc_h), (1, vc_h))]
+            own_out = [pltpu.make_async_copy(own.at[t], block(t, me), osem.at[1, t]) for t in range(2)]
+            own_ring = [remote(own.at[t], block(t, me), rs.at[t], rr.at[t], succ) for t in range(2)]
+            own_part = [remote(own.at[t], block(t, me), ps.at[t], pr.at[t], partner) for t in range(2)]
+
+            def fwd_ring(a):
+                return remote(block(a % 2, mine(a)), block(a % 2, mine(a)), rs.at[a + 2], rr.at[a + 2], succ)
+
+            def fwd_part(a):
+                return remote(block(a % 2, mine(a)), block(a % 2, mine(a)), ps.at[a + 2], pr.at[a + 2], partner)
+
+            def handle(a):
+                remote(block(a % 2, mine(a)), block(a % 2, mine(a)), rs.at[a], rr.at[a], pred).wait_recv()
+
+                @pl.when(a + 2 < n_arr)
+                def _():
+                    fwd_ring(a).start()
+                fwd_part(a).start()
+
+            halo = [remote(kvx.at[t, pl.ds(rows, rows), :], kvx.at[t, pl.ds(0, rows), :], hsem.at[0, t], hsem.at[1, t], me + 1) for t in range(2)]
+            halo_in = [remote(kvx.at[t, pl.ds(rows, rows), :], kvx.at[t, pl.ds(0, rows), :], hsem.at[0, t], hsem.at[1, t], me - 1) for t in range(2)]
+            first_in = [pltpu.make_async_copy(src.at[pair], kvx.at[t, pl.ds(0, rows), :], hsem.at[1, t]) for t, src in ((0, kl_h), (1, vl_h))]
+
+            for c in own_in:
                 c.start()
-        if "oproj" not in names and "mlp" not in names:
-            xs_src = x_ref
-        else:
-            xs_src = None
-        cur = [x_ref]
+            barrier = pltpu.get_barrier_semaphore()
+            for who in (pred, partner):
+                pl.semaphore_signal(barrier, inc=1, device_id={"ctx": who}, device_id_type=MESH)
+
+            @pl.when(p == 0)
+            def _():
+                pl.semaphore_signal(barrier, inc=1, device_id={"ctx": (me - 1 + n_ctx) % n_ctx}, device_id_type=MESH)
+
+            @pl.when(me == 0)
+            def _():
+                for c in first_in:
+                    c.start()
+            pl.semaphore_wait(barrier, 2 + p)
+            for t in range(2):
+                own_in[t].wait()
+                own_ring[t].start()
+                own_part[t].start()
+                own_out[t].start()
 
         def do_lattn(l):
             half = rows // 2
-            sc["kx"][0:rows, :] = hk_ref[...]
-            sc["kx"][rows:2 * rows, :] = k_ref[...]
-            sc["vx"][0:rows, :] = hv_ref[...]
-            sc["vx"][rows:2 * rows, :] = v_ref[...]
+
+            @pl.when(me == 0)
+            def _():
+                for c in first_in:
+                    c.wait()
+
+            @pl.when(me > 0)
+            def _():
+                for c in halo_in:
+                    c.wait_recv()
             span = rows + half
             ri = lax.broadcasted_iota(jnp.int32, (half, span), 0)
             ci = lax.broadcasted_iota(jnp.int32, (half, span), 1)
             ok = (ci > ri) & (ci <= ri + rows)
             for t in range(2):
                 for h in range(heads):
-                    qt = q_ref[t * half:(t + 1) * half, h * kw:(h + 1) * kw]
-                    s = dot_t(qt, sc["kx"][t * half:t * half + span, :])
-                    s = jnp.where(ok, s, NEG)
+                    qt = qs[t * half:(t + 1) * half, h * kw:(h + 1) * kw]
+                    s = dot_t(qt, kvx[0, t * half:t * half + span, :])
+                    s = jnp.where(ok, s, -jnp.inf)
                     m = jnp.max(s, axis=1, keepdims=True)
-                    p = jnp.exp2((s - m) * scale)
-                    den = jnp.sum(p, axis=1, keepdims=True)
-                    num = dotf(p.astype(jnp.bfloat16), sc["vx"][t * half:t * half + span, :])
+                    e = jnp.exp2((s - m) * scale)
+                    den = jnp.sum(e, axis=1, keepdims=True)
+                    num = dotf(e.astype(jnp.bfloat16), kvx[1, t * half:t * half + span, :])
                     os_[t * half:(t + 1) * half, h * kw:(h + 1) * kw] = (num / den).astype(jnp.bfloat16)
 
         def do_oproj(l):
-            src = os_ if has_l else a_ref
+            src = a_ref if attn is not None and l == oprojs[0] else os_
             o_copy(l).wait()
             xs[...] = (cur[0][...].astype(jnp.float32) + dotf(src[...], sc["wob"][...])).astype(jnp.bfloat16)
             cur[0] = xs
+            if l != oprojs[-1]:
+                o_copy(oprojs[-1]).start()
 
         def do_mlp(l):
             hs[...] = rms_rows(cur[0][...], gm_ref[l:l + 1, :])
@@ -166,11 +251,23 @@
                 a = (jax.nn.gelu(ga, approximate=True) * up).astype(jnp.bfloat16)
                 acc[...] += dotf(a, sc["wdb"][slot])
 
-            def loop(jj, _):
-                for s in range(NS):
-                    step(jj * NS + s, s, (s + NS - 1) % NS)
+            base = sent[0]
+
+            def loop(j, _):
+                step(j, lax.rem(j, NS), lax.rem(j + NS - 1, NS))
+                if has_l:
+                    @pl.when(j + base < n_arr)
+                    def _():
+                        handle(j + base)
                 return 0
-            lax.fori_loop(0, nb // NS, loop, 0)
+            lax.fori_loop(0, nb, loop, 0)
+            sent[0] = min(base + nb, n_arr)
+            if has_l and l == mlps[-1]:
+                for a in range(sent[0], n_arr):
+                    handle(a)
+                sent[0] = n_arr
+            if l != mlps[-1]:
+                start_mlp(mlps[-1])
             xs[...] = acc[...].astype(jnp.bfloat16)
             cur[0] = xs
 
@@ -178,25 +275,74 @@
             hs[...] = rms_rows(cur[0][...], ga_ref[l:l + 1, :])
             for c in qkv_copies(l):
                 c.wait()
-            o_refs[2][...] = dotf(hs[...], sc["wkb"][...]).astype(jnp.bfloat16)
-            o_refs[3][...] = dotf(hs[...], sc["wvb"][...]).astype(jnp.bfloat16)
-            o_refs[1][...] = dotf(hs[...], sc["wqb"][...]).astype(jnp.bfloat16)
-
+            to_local = has_l and l == qkvs[0]
+            if to_local:
+                kvx[0, rows:2 * rows, :] = dotf(hs[...], sc["wkb"][...]).astype(jnp.bfloat16)
+                kvx[1, rows:2 * rows, :] = dotf(hs[...], sc["wvb"][...]).astype(jnp.bfloat16)
+
+                @pl.when(me < n_ctx - 1)
+                def _():
+                    halo[0].start()
+                half_q = qw // 2
+                qs[:, 0:half_q] = dotf(hs[...], sc["wqb"][:, 0:half_q]).astype(jnp.bfloat16)
+
+                @pl.when(me < n_ctx - 1)
+                def _():
+                    halo[1].start()
+                qs[:, half_q:qw] = dotf(hs[...], sc["wqb"][:, half_q:qw]).astype(jnp.bfloat16)
+                for c in qkv_copies(qkvs[1]):
+                    c.start()
+            else:
+                o_refs[2][...] = dotf(hs[...], sc["wkb"][...]).astype(jnp.bfloat16)
+                o_refs[3][...] = dotf(hs[...], sc["wvb"][...]).astype(jnp.bfloat16)
+                o_refs[1][...] = dotf(hs[...], sc["wqb"][...]).astype(jnp.bfloat16)
+
+        early = 4 if attn is None else 0
         for s, l in stages:
             dict(lattn=do_lattn, oproj=do_oproj, mlp=do_mlp, qkv=do_qkv)[s](l)
+            if early and s == "qkv" and sent[0] == 0:
+                handle(0)
+                sent[0] = 1
+            if early and s == "oproj":
+                for a in range(sent[0], early):
+                    handle(a)
+                sent[0] = early
         o_refs[0][...] = cur[0][...]
+        if has_l:
+            for t in range(2):
+                own_ring[t].wait_send()
+                own_part[t].wait_send()
+                own_out[t].wait()
+
+            @pl.when(me < n_ctx - 1)
+            def _():
+                for c in halo:
+                    c.wait_send()
+
+            def drain(a, carry):
+                @pl.when(a + 2 < n_arr)
+                def _():
+                    fwd_ring(a).wait_send()
+                fwd_part(a).wait_send()
+                return carry
+            lax.fori_loop(0, n_arr, drain, 0)
+
+            def arrive(a, carry):
+                d = theirs(a)
+                remote(block(a % 2, d), block(a % 2, d), ps.at[a], pr.at[a], partner).wait_recv()
+                return carry
+            lax.fori_loop(0, n_arr + 2, arrive, 0)
 
     flops = 0
     for s, l in stages:
         flops += 2 * rows * width * {"mlp": 3 * ff, "qkv": qw + 2 * kw, "oproj": qw, "lattn": 4 * rows}[s]
     return pl.pallas_call(
-        kernel, out_shape=tuple(outs), in_specs=specs, out_specs=tuple([vm] * len(outs)),
+        kernel, out_shape=tuple(outs), in_specs=specs, out_specs=tuple(out_specs),
         scratch_shapes=list(scratch.values()),
         cost_estimate=pl.CostEstimate(flops=flops, bytes_accessed=len(mlps) * 3 * width * ff * 2 + 10**6, transcendentals=0),
-        compiler_params=pltpu.CompilerParams(vmem_limit_bytes=60 * 1024 * 1024), name=name)(*ins)
-
-
-MESH = pl.DeviceIdType.MESH
+        compiler_params=pltpu.CompilerParams(vmem_limit_bytes=60 * 1024 * 1024, collective_id=cid, has_side_effects=cid is not None), name=name)(*ins)
+
+
 CB = 1024
 
 
@@ -230,28 +376,28 @@
             acc_ref[:, lo:lo + 128] = acc_ref[:, lo:lo + 128] * alpha + pv[:, c * 128:(c + 1) * 128]
 
 
-def global_call(q, k, v, ck, cv, clen, n_ctx, heads=4):
+def global_call(q, k, v, cc, clen, n_ctx, heads=4):
     rows, qw = q.shape
     dim = k.shape[1]
-    slots = ck.shape[0]
+    slots = cc.shape[1]
     ncb = slots // CB
     n_chip = n_ctx // 2
     scale = dim ** -0.5 * LOG2E
     n_arr = 2 * (n_chip - 1)
 
-    def kernel(clen_ref, q_ref, k_ref, v_ref, ck_h, cv_h, o_ref, kv, m_ref, l_ref, acc_ref, s_scr, cb, csem, rs, rr, ps, pr):
+    def kernel(clen_ref, q_ref, k_ref, v_ref, cc_h, o_ref, kv, m_ref, l_ref, acc_ref, s_scr, cb, csem, rs, rr, ps, pr):
         me = lax.axis_index("ctx")
         z, p = me // 2, me % 2
-        step_dir = 1 - 2 * p
+        way = 1 - 2 * p
         partner = z * 2 + (1 - p)
-        succ = ((z + step_dir + n_chip) % n_chip) * 2 + p
-        pred = ((z - step_dir + n_chip) % n_chip) * 2 + p
+        succ = ((z + way + n_chip) % n_chip) * 2 + p
+        pred = ((z - way + n_chip) % n_chip) * 2 + p
 
         def mine(s):
-            return ((z - step_dir * s + n_chip) % n_chip) * 2 + p
+            return ((z - way * s + n_chip) % n_chip) * 2 + p
 
         def theirs(s):
-            return ((z + step_dir * s + n_chip) % n_chip) * 2 + (1 - p)
+            return ((z + way * s + n_chip) % n_chip) * 2 + (1 - p)
 
         barrier = pltpu.get_barrier_semaphore()
         for who in (pred, partner):
@@ -290,7 +436,7 @@
 
         def ccopy(i):
             off = pl.multiple_of(i * CB, CB)
-            return [pltpu.make_async_copy(src.at[pl.ds(off, CB), :], cb.at[t, i % 2], csem.at[t, i % 2]) for t, src in ((0, ck_h), (1, cv_h))]
+            return [pltpu.make_async_copy(cc_h.at[t, pl.ds(off, CB), :], cb.at[t, i % 2], csem.at[t, i % 2]) for t in range(2)]
 
         for c in ccopy(0):
             c.start()
@@ -329,20 +475,27 @@
             def _():
                 units(lambda: kv[0, d], lambda: kv[1, d], rows, None)
 
-        wait_partner(0, 0)
-        wait_partner(1, 0)
-        shard(partner)
-
-        def new_step(s, carry):
-            @pl.when(s + ncb - 2 < n_arr)
-            def _():
-                handle(s + ncb - 2)
-            shard(mine(s))
-            wait_partner(0, s)
-            wait_partner(1, s)
-            shard(theirs(s))
+        def new_step(j, carry):
+            s = (j + 1) // 2
+            odd = j % 2
+            d = ((z + way * (1 - 2 * odd) * s + n_chip) % n_chip) * 2 + (p + 1 - odd) % 2
+
+            @pl.when(odd == 1)
+            def _():
+                @pl.when(s + ncb - 2 < n_arr)
+                def _():
+                    handle(s + ncb - 2)
+
+            @pl.when(odd == 0)
+            def _():
+                wait_partner(0, s)
+                wait_partner(1, s)
+
+            @pl.when(d < me)
+            def _():
+                units(lambda: kv[0, d], lambda: kv[1, d], rows, None)
             return carry
-        lax.fori_loop(1, n_chip, new_step, 0)
+        lax.fori_loop(0, n_ctx - 1, new_step, 0)
 
         for t in range(2):
             own_send(t, succ, rs, rr, t).wait_send()
@@ -364,7 +517,7 @@
     sem = pltpu.SemaphoreType.DMA
     return pl.pallas_call(
         kernel, out_shape=jax.ShapeDtypeStruct((rows, qw), jnp.bfloat16),
-        in_specs=[pl.BlockSpec(memory_space=pltpu.SMEM), vm, vm, vm, hb, hb], out_specs=vm,
+        in_specs=[pl.BlockSpec(memory_space=pltpu.SMEM), vm, vm, vm, hb], out_specs=vm,
         scratch_shapes=[
             pltpu.VMEM((2, n_ctx, rows, dim), jnp.bfloat16),
             pltpu.VMEM((heads, rows, 128), jnp.float32), pltpu.VMEM((heads, rows, 128), jnp.float32),
@@ -372,12 +525,11 @@
             pltpu.VMEM((2, 2, CB, dim), jnp.bfloat16), sem((2, 2)),
             sem((n_arr,)), sem((n_arr,)), sem((n_arr + 2,)), sem((n_arr + 2,))],
         cost_estimate=pl.CostEstimate(flops=4 * rows * qw * (slots + n_ctx * rows), bytes_accessed=4 * slots * dim, transcendentals=0),
-        compiler_params=pltpu.CompilerParams(vmem_limit_bytes=60 * 1024 * 1024, collective_id=1, has_side_effects=True), name="gattn")(clen, q, k, v, ck, cv)
+        compiler_params=pltpu.CompilerParams(vmem_limit_bytes=60 * 1024 * 1024, collective_id=1, has_side_effects=True), name="gattn")(clen, q, k, v, cc)
 
 
 def solution(mesh):
     n_ctx = mesh.shape['ctx']
-    shift_pairs = [(i, i + 1) for i in range(n_ctx - 1)]
     row_spec = P(('dp', 'ctx'), None)
     cache_spec = P(None, ('dp', 'ctx'), None, None)
     local_spec = P(None, 'dp', None, None)
@@ -385,21 +537,18 @@
 
     def device_step(x, cache_len, k_cache, v_cache, k_local, v_local, g_attn, g_mlp, w_q, w_k, w_v, w_o, w_gate, w_up, w_down):
         weights = (g_attn, g_mlp, w_q, w_k, w_v, w_o, w_gate, w_up, w_down)
-        is_first = lax.axis_index('ctx') == 0
         n_pairs = k_cache.shape[0]
-        caches = [[lax.all_gather(c[i, :, 0, :], 'ctx', axis=0, tiled=True) for c in (k_cache, v_cache)] for i in range(n_pairs)]
-        _, q, k, v = dense_call([("qkv", 0)], x, weights, name="qkv")
+        flat = lambda a: a.reshape(a.shape[0], a.shape[1], a.shape[2] * a.shape[3])
+        local = (flat(k_local), flat(v_local))
+        caches = (flat(k_cache), flat(v_cache))
+        o = None
         for i in range(n_pairs):
-            halo_k = jnp.where(is_first, k_local[i, :, 0, :], lax.ppermute(k, 'ctx', shift_pairs))
-            halo_v = jnp.where(is_first, v_local[i, :, 0, :], lax.ppermute(v, 'ctx', shift_pairs))
             l = 2 * i
-            x, q, k, v = dense_call([("lattn", l), ("oproj", l), ("mlp", l), ("qkv", l + 1)], x, weights, q=q, k=k, v=v, halo_k=halo_k, halo_v=halo_v, name="local%d" % i)
-            o = global_call(q, k, v, caches[i][0], caches[i][1], cache_len, n_ctx)
-            last = i == n_pairs - 1
-            r = dense_call([("oproj", l + 1), ("mlp", l + 1)] + ([] if last else [("qkv", l + 2)]), x, weights, attn=o, name="glob%d" % i)
-            x = r[0]
-            if not last:
-                q, k, v = r[1:]
-        return x
+            head = [] if i == 0 else [("oproj", l - 1), ("mlp", l - 1)]
+            stages = head + [("qkv", l), ("lattn", l), ("oproj", l), ("mlp", l), ("qkv", l + 1)]
+            x, q, k, v, cc = dense_call(stages, x, weights, local=local, caches=caches, pair=i, attn=o, n_ctx=n_ctx, cid=2 + i, name="dense%d" % i)
+            o = global_call(q, k, v, cc, cache_len, n_ctx)
+        l = 2 * n_pairs - 1
+        return dense_call([("oproj", l), ("mlp", l)], x, weights, attn=o, name="last")[0]
 
     return jax.shard_map(device_step, mesh=mesh, in_specs=in_specs, out_specs=row_spec, check_vma=False)

time: 391 us -> 315 us (0.81)
  waiting for transfers between devices: 27 us -> 0 us
  Pallas kernels: 323 us -> 309 us
  starting transfers between devices: 13.6 us -> 0 us
  between operations: 14.2 us -> 1.15 us
    pallas_call x2, Pallas kernels: 144 us -> 115 us  [global_call(): pl.pallas_call(kernel, out_shape=jax.ShapeDtypeStruct((rows, qw), jnp.bfl...]
    pallas_call x5 -> x3, Pallas kernels: 179 us -> 194 us  [dense_call(): pl.pallas_call(kernel, out_shape=tuple(outs), in_specs=specs, out_specs=t...]
    ppermute x4 -> x0, starting transfers between devices: 13.4 us -> none  [the longest x2 9.34 us: device_step(): lax.ppermute(k, 'ctx', shift_pairs)]
    ppermute x4 -> x0, waiting for transfers between devices: 13.4 us -> none  [the longest x2 9.72 us: device_step(): lax.ppermute(v, 'ctx', shift_pairs)]
    all_gather x4 -> x0, waiting for transfers between devices: 12.8 us -> none  [device_step(): lax.all_gather(c[i, :, 0, :], 'ctx', axis=0, tiled=True)]
  transfers between devices with their start and end apart: 8 -> 0, of which waited for: 5 -> 0; matrix products, arithmetic and copies ran while one was open for 1% -> 0% of each run, Pallas kernels for 59% -> 0%
where the time goes in v2:
time: 315 us; the launch traced here: 310 us
  Pallas kernels  309 us (98%)
    pallas_call x3, Pallas kernels, dense_call(): pl.pallas_call(kernel, out_shape=tuple(outs), in_specs=specs, out_specs=t...  194 us
    pallas_call x2, Pallas kernels, global_call(): pl.pallas_call(kernel, out_shape=jax.ShapeDtypeStruct((rows, qw), jnp.bfl...  115 us

profile of v2, /device:TPU:21, one launch (start us, length us, event | category | flops | bytes accessed | tf_op | source)
XLA Modules:
  0.0 310.3 jit_solution(4282073758432112672)
XLA Ops:
  0.7 72.7 %dense0.1 = (bf16[512,1152]{1,0:T(8,128)(2,1)}, bf16[512,1024]{1,0:T(8,128)(2,1)}, bf16[512,256]{1,0:T(8,128)(2,1)}, bf16[512,256]{1,0:T(8,128)(2,1)}, bf16[2,8192,256]{2,1,0:T(8,128)(2,1)}) custom-call(bf16[512,1152]{1,0:T(8,128)(2,1)} %refs_0_.1, bf16[4,1152]{1,0:T(4,128)(2,1)} %refs_1_.5, bf16[4,1152]{1,0:T(4,128)(2,1)} %refs_2_.5, ...), custom_call_target="tpu_custom_call" | custom-call | flops 31708938240 | bytes 48775744 | tf_op jit(solution)/shard_map/dense0/pallas_call | solution.py:339
  73.4 56.1 %gattn.2.refs_3_ = bf16[512,1024]{1,0:T(8,128)(2,1)} custom-call(s32[1]{0:T(128)S(6)} %copy.16.clen_ref, bf16[512,1024]{1,0:T(8,128)(2,1)} %get-tuple-element.16.q_ref, bf16[512,256]{1,0:T(8,128)(2,1)} %get-tuple-element.17.k_ref, bf16[512,256]{1,0:T(8,128)(2,1)} %get-tuple-element.18.v_ref, bf16[2,8192,256]{2,1,0:T(8,128)(2,1)} %get-tuple-element.19.cc_h), custom_call_target="tpu_custom_call" | custom-call | flops 34359738368 | bytes 8388608 | tf_op jit(solution)/shard_map/gattn/pallas_call | solution.py:518
  129.5 84.4 %dense1.1 = (bf16[512,1152]{1,0:T(8,128)(2,1)}, bf16[512,1024]{1,0:T(8,128)(2,1)}, bf16[512,256]{1,0:T(8,128)(2,1)}, bf16[512,256]{1,0:T(8,128)(2,1)}, bf16[2,8192,256]{2,1,0:T(8,128)(2,1)}) custom-call(bf16[512,1152]{1,0:T(8,128)(2,1)} %get-tuple-element.15.refs_0_, bf16[4,1152]{1,0:T(4,128)(2,1)} %refs_1_.5, bf16[4,1152]{1,0:T(4,128)(2,1)} %refs_2_.5, ...), custom_call_target="tpu_custom_call" | custom-call | flops 57378078720 | bytes 96551488 | tf_op jit(solution)/shard_map/dense1/pallas_call | solution.py:339
  214.0 59.3 %gattn.3.refs_3_ = bf16[512,1024]{1,0:T(8,128)(2,1)} custom-call(s32[1]{0:T(128)S(6)} %copy.16.clen_ref, bf16[512,1024]{1,0:T(8,128)(2,1)} %get-tuple-element.21.q_ref, bf16[512,256]{1,0:T(8,128)(2,1)} %get-tuple-element.22.k_ref, bf16[512,256]{1,0:T(8,128)(2,1)} %get-tuple-element.23.v_ref, bf16[2,8192,256]{2,1,0:T(8,128)(2,1)} %get-tuple-element.24.cc_h), custom_call_target="tpu_custom_call" | custom-call | flops 34359738368 | bytes 8388608 | tf_op jit(solution)/shard_map/gattn/pallas_call | solution.py:518
  273.3 36.5 %last.1 = bf16[512,1152]{1,0:T(8,128)(2,1)} custom-call(bf16[512,1152]{1,0:T(8,128)(2,1)} %get-tuple-element.20.refs_0_, bf16[4,1152]{1,0:T(4,128)(2,1)} %refs_1_.5, bf16[4,1152]{1,0:T(4,128)(2,1)} %refs_2_.5, bf16[512,1024]{1,0:T(8,128)(2,1)} %gattn.3.refs_3_, bf16[4,1152,1024]{2,1,0:T(8,128)(2,1)} %refs_4_.5, bf16[4,1152,256]{2,1,0:T(8,128)(2,1)} %refs_5_.5, ...), custom_call_target="tpu_custom_call" | custom-call | flops 25669140480 | bytes 48775744 | tf_op jit(solution)/shard_map/last/pallas_call | solution.py:339

commit v3 on v2

--- a/solution.py
+++ b/solution.py
@@ -211,6 +211,9 @@
             def _():
                 for c in halo_in:
                     c.wait_recv()
+            if sent[0] == 1:
+                handle(1)
+                sent[0] = 2
             span = rows + half
             ri = lax.broadcasted_iota(jnp.int32, (half, span), 0)
             ci = lax.broadcasted_iota(jnp.int32, (half, span), 1)
@@ -263,9 +266,9 @@
             lax.fori_loop(0, nb, loop, 0)
             sent[0] = min(base + nb, n_arr)
             if has_l and l == mlps[-1]:
-                for a in range(sent[0], n_arr):
+                for a in range(sent[0], n_arr - 1):
                     handle(a)
-                sent[0] = n_arr
+                sent[0] = max(sent[0], n_arr - 1)
             if l != mlps[-1]:
                 start_mlp(mlps[-1])
             xs[...] = acc[...].astype(jnp.bfloat16)
@@ -297,18 +300,16 @@
                 o_refs[3][...] = dotf(hs[...], sc["wvb"][...]).astype(jnp.bfloat16)
                 o_refs[1][...] = dotf(hs[...], sc["wqb"][...]).astype(jnp.bfloat16)
 
-        early = 4 if attn is None else 0
+        early = 3 if attn is None else 0
         for s, l in stages:
             dict(lattn=do_lattn, oproj=do_oproj, mlp=do_mlp, qkv=do_qkv)[s](l)
-            if early and s == "qkv" and sent[0] == 0:
-                handle(0)
-                sent[0] = 1
-            if early and s == "oproj":
-                for a in range(sent[0], early):
-                    handle(a)
-                sent[0] = early
+            if sent[0] < early and s in ("qkv", "oproj"):
+                handle(sent[0])
+                sent[0] += 1
         o_refs[0][...] = cur[0][...]
         if has_l:
+            for a in range(sent[0], n_arr):
+                handle(a)
             for t in range(2):
                 own_ring[t].wait_send()
                 own_part[t].wait_send()

time: 315 us -> 312 us (level)
  no operation moved by 1% of the time
where the time goes in v3:
time: 312 us; the launch traced here: 307 us
  Pallas kernels  306 us (98%)
    pallas_call x3, Pallas kernels, dense_call(): pl.pallas_call(kernel, out_shape=tuple(outs), in_specs=specs, out_specs=t...  192 us
    pallas_call x2, Pallas kernels, global_call(): pl.pallas_call(kernel, out_shape=jax.ShapeDtypeStruct((rows, qw), jnp.bfl...  114 us

profile of v3, /device:TPU:21, one launch (start us, length us, event | category | flops | bytes accessed | tf_op | source)
XLA Modules:
  0.0 306.8 jit_solution(9627068550276234160)
XLA Ops:
  0.7 70.9 %dense0.1 = (bf16[512,1152]{1,0:T(8,128)(2,1)}, bf16[512,1024]{1,0:T(8,128)(2,1)}, bf16[512,256]{1,0:T(8,128)(2,1)}, bf16[512,256]{1,0:T(8,128)(2,1)}, bf16[2,8192,256]{2,1,0:T(8,128)(2,1)}) custom-call(bf16[512,1152]{1,0:T(8,128)(2,1)} %refs_0_.1, bf16[4,1152]{1,0:T(4,128)(2,1)} %refs_1_.5, bf16[4,1152]{1,0:T(4,128)(2,1)} %refs_2_.5, ...), custom_call_target="tpu_custom_call" | custom-call | flops 31708938240 | bytes 48775744 | tf_op jit(solution)/shard_map/dense0/pallas_call | solution.py:340
  71.6 54.2 %gattn.2.refs_3_ = bf16[512,1024]{1,0:T(8,128)(2,1)} custom-call(s32[1]{0:T(128)S(6)} %copy.16.clen_ref, bf16[512,1024]{1,0:T(8,128)(2,1)} %get-tuple-element.16.q_ref, bf16[512,256]{1,0:T(8,128)(2,1)} %get-tuple-element.17.k_ref, bf16[512,256]{1,0:T(8,128)(2,1)} %get-tuple-element.18.v_ref, bf16[2,8192,256]{2,1,0:T(8,128)(2,1)} %get-tuple-element.19.cc_h), custom_call_target="tpu_custom_call" | custom-call | flops 34359738368 | bytes 8388608 | tf_op jit(solution)/shard_map/gattn/pallas_call | solution.py:519
  125.8 84.7 %dense1.1 = (bf16[512,1152]{1,0:T(8,128)(2,1)}, bf16[512,1024]{1,0:T(8,128)(2,1)}, bf16[512,256]{1,0:T(8,128)(2,1)}, bf16[512,256]{1,0:T(8,128)(2,1)}, bf16[2,8192,256]{2,1,0:T(8,128)(2,1)}) custom-call(bf16[512,1152]{1,0:T(8,128)(2,1)} %get-tuple-element.15.refs_0_, bf16[4,1152]{1,0:T(4,128)(2,1)} %refs_1_.5, bf16[4,1152]{1,0:T(4,128)(2,1)} %refs_2_.5, ...), custom_call_target="tpu_custom_call" | custom-call | flops 57378078720 | bytes 96551488 | tf_op jit(solution)/shard_map/dense1/pallas_call | solution.py:340
  210.5 59.3 %gattn.3.refs_3_ = bf16[512,1024]{1,0:T(8,128)(2,1)} custom-call(s32[1]{0:T(128)S(6)} %copy.16.clen_ref, bf16[512,1024]{1,0:T(8,128)(2,1)} %get-tuple-element.21.q_ref, bf16[512,256]{1,0:T(8,128)(2,1)} %get-tuple-element.22.k_ref, bf16[512,256]{1,0:T(8,128)(2,1)} %get-tuple-element.23.v_ref, bf16[2,8192,256]{2,1,0:T(8,128)(2,1)} %get-tuple-element.24.cc_h), custom_call_target="tpu_custom_call" | custom-call | flops 34359738368 | bytes 8388608 | tf_op jit(solution)/shard_map/gattn/pallas_call | solution.py:519
  269.9 36.5 %last.1 = bf16[512,1152]{1,0:T(8,128)(2,1)} custom-call(bf16[512,1152]{1,0:T(8,128)(2,1)} %get-tuple-element.20.refs_0_, bf16[4,1152]{1,0:T(4,128)(2,1)} %refs_1_.5, bf16[4,1152]{1,0:T(4,128)(2,1)} %refs_2_.5, bf16[512,1024]{1,0:T(8,128)(2,1)} %gattn.3.refs_3_, bf16[4,1152,1024]{2,1,0:T(8,128)(2,1)} %refs_4_.5, bf16[4,1152,256]{2,1,0:T(8,128)(2,1)} %refs_5_.5, ...), custom_call_target="tpu_custom_call" | custom-call | flops 25669140480 | bytes 48775744 | tf_op jit(solution)/shard_map/last/pallas_call | solution.py:340
